TPU v7x, 256 devices: a whole 4x4x8 slice. The times are simulated.
256 devices in a mesh: sector: 16 (over z, core), term: 16 (over y, x).
Axes of the slice: x: 4, y: 4, z: 8, core: 2. Of those that a mesh axis runs over, the one named last changes fastest.
Arguments:
- psi: bfloat16 [256, 256, 256], P('sector'), may hold values from -6 to 6
- sector_sizes: int32 [256], P('sector'), may hold values from 64 to 256, as said below
- left_env: bfloat16 [768, 16, 256, 256], P('term', 'sector'), may hold values from -0.0546875 to 0.0546875
- right_env: bfloat16 [768, 16, 256, 256], P('term', 'sector'), may hold values from -0.375 to 0.375
- target: int32 [768, 16], P('term', 'sector'), may hold values from 0 to 255, as said below
- source: int32 [768, 16], P('term', 'sector'), may hold values from 0 to 255, as said below
- live_count: int32 [16, 16], P('term', 'sector'), may hold values from 1 to 48, as said below
Outputs:
- sigma: float32 [256, 256, 256], P('sector', 'term')
Inputs may be any that keep to these rules, and one draw needn't show every extreme that they name: target[j, g] lies among the sectors of sector group g, from g * 16 to (g + 1) * 16 - 1. source[j, g] differs from target[j, g] by at most 16. `live_count`: some device has all 48 slots live in every draw. `sector_sizes`: some sector has all 256 rows live in every draw.
All inputs are finite; a program needn't handle non-finite values.
Results may differ from a plain program's by a relative error of at most 0.0042.
Values may be sent and summed in bfloat16 or wider, within the bound.
No kernel may reach another device: no remote copies, remote signals or barrier semaphores. Data moves between devices by JAX's collectives and lax.ppermute only.
A program may use at most 128 MiB of HBM per device.

v0:
```python
import jax
import jax.numpy as jnp
from jax import lax
from jax.sharding import PartitionSpec as P


def extended(x, sides, width):
    for axis, dim in sides:
        devices, length = (lax.axis_size(axis), x.shape[dim])
        up = [(i, (i + 1) % devices) for i in range(devices - 1)]
        down = [(j, i) for i, j in up]
        last = lax.slice_in_dim(x, length - width, length, axis=dim)
        leading = lax.slice_in_dim(x, 0, width, axis=dim)
        before = lax.ppermute(last, axis, up)
        after = lax.ppermute(leading, axis, down)
        x = jnp.concatenate([before, x, after], axis=dim)
    return x


def cut_along(x, dim, devices):
    before, after = (x.shape[:dim], x.shape[dim + 1 :])
    return jnp.moveaxis(x.reshape(*before, devices, -1, *after), dim, 0)


def sum_at_owner(x, axis, dim):
    devices = lax.axis_size(axis)
    tiles = lax.all_to_all(cut_along(x, dim, devices), axis, 0, 0, tiled=True)
    return jnp.sum(tiles.astype(jnp.float32), axis=0)


def on_device(psi, sector_sizes, left_env, right_env, target, source, live_count):
    sec_count = psi.shape[0]
    block = psi.shape[1]
    slot_count = left_env.shape[0]
    group = lax.axis_index("sector")
    index_row = jnp.arange(block, dtype=jnp.int32)
    keep = (index_row[None, :, None] < sector_sizes[:, None, None]) & (
        index_row[None, None, :] < sector_sizes[:, None, None]
    )
    masked = jnp.where(keep, psi, jnp.zeros_like(psi))
    left = left_env[:, 0]
    right = right_env[:, 0]
    tgt = target[:, 0]
    src = source[:, 0]
    nearby = extended(masked, (("sector", 0),), sec_count)
    local_src = src - (group * sec_count - sec_count)
    picked = jnp.take(nearby, local_src, axis=0)
    inner = jnp.einsum("jab,jbc->jac", left, picked, preferred_element_type=jnp.float32).astype(
        jnp.bfloat16
    )
    contribution = jnp.einsum("jac,jdc->jad", inner, right, preferred_element_type=jnp.float32)
    alive = (jnp.arange(slot_count, dtype=jnp.int32) < live_count[0, 0]).astype(jnp.float32)
    selector = (
        (tgt - group * sec_count)[:, None] == jnp.arange(sec_count, dtype=jnp.int32)[None, :]
    ).astype(jnp.float32)
    selector = selector * alive[:, None]
    partial_sums = jnp.einsum(
        "js,jad->sad", selector, contribution, precision=lax.Precision.HIGHEST
    )
    partial_sums = jnp.where(keep, partial_sums, jnp.zeros_like(partial_sums))
    return sum_at_owner(partial_sums.astype(jnp.bfloat16), "term", 1)


def solution(mesh):
    placed = (
        P("sector", None, None),
        P("sector"),
        P("term", "sector", None, None),
        P("term", "sector", None, None),
        P("term", "sector"),
        P("term", "sector"),
        P("term", "sector"),
    )
    return jax.shard_map(
        on_device, mesh=mesh, in_specs=placed, out_specs=P("sector", "term", None), check_vma=False
    )
```

profile of v0, /device:TPU:161, one launch (start us, length us, event | category | flops | bytes accessed | tf_op | source)
XLA Modules:
  0.0 119.8 jit_solution(9330268944093411917)
XLA Ops:
  0.0 0.7 iota_compare_fusion
  0.7 0.1 copy.13
  0.9 6.2 %and_select_fusion.1 = bf16[16,256,256]{2,0,1:T(8,128)(2,1)S(1)} fusion(bf16[16,256,256]{2,1,0:T(8,128)(2,1)} %param.7, pred[16,256]{1,0:T(8,128)(4,1)S(1)} %iota_compare_fusion, pred[16,256]{0,1:T(8,128)(4,1)S(1)} %copy.13), kind=kLoop, calls=%fused_computation.12 | loop fusion | flops 2097152 | bytes 4202496 | tf_op jit(solution)/shard_map/jit(_where)/select_n | solution.py:40
  7.1 3.2 %collective-permute-start = (bf16[16,256,256]{2,0,1:T(8,128)(2,1)S(1)}, bf16[16,256,256]{2,0,1:T(8,128)(2,1)}, u32[]{:S(2)}, u32[]{:S(2)}) collective-permute-start(bf16[16,256,256]{2,0,1:T(8,128)(2,1)S(1)} %and_select_fusion.1), channel_id=1, source_target_pairs={{0,16},{16,32},{32,48},{48,64},{64,80},{80,96},{96,112},{112,128},... | collective-permute-start | bytes 6291464 | tf_op jit(solution)/shard_map/ppermute | solution.py:14
  10.3 1.9 %collective-permute-start.1 = (bf16[16,256,256]{2,0,1:T(8,128)(2,1)S(1)}, bf16[16,256,256]{2,0,1:T(8,128)(2,1)}, u32[]{:S(2)}, u32[]{:S(2)}) collective-permute-start(bf16[16,256,256]{2,0,1:T(8,128)(2,1)S(1)} %and_select_fusion.1), channel_id=1, source_target_pairs={{16,0},{32,16},{48,32},{64,48},{80,64},{96,80},{112,96},{128,112},... | collective-permute-start | bytes 6291464 | tf_op jit(solution)/shard_map/ppermute | solution.py:15
  12.9 0.7 and_bitcast_fusion
  13.6 0.7 subtract_bitcast_fusion
  14.2 19.0 %collective-permute-done = bf16[16,256,256]{2,0,1:T(8,128)(2,1)} collective-permute-done((bf16[16,256,256]{2,0,1:T(8,128)(2,1)S(1)}, bf16[16,256,256]{2,0,1:T(8,128)(2,1)}, u32[]{:S(2)}, u32[]{:S(2)}) %collective-permute-start) | collective-permute-done | bytes 2097184 | tf_op jit(solution)/shard_map/ppermute | solution.py:14
  33.2 4.5 %collective-permute-done.1 = bf16[16,256,256]{2,0,1:T(8,128)(2,1)} collective-permute-done((bf16[16,256,256]{2,0,1:T(8,128)(2,1)S(1)}, bf16[16,256,256]{2,0,1:T(8,128)(2,1)}, u32[]{:S(2)}, u32[]{:S(2)}) %collective-permute-start.1) | collective-permute-done | bytes 2097184 | tf_op jit(solution)/shard_map/ppermute | solution.py:15
  37.8 3.0 %pad_maximum_fusion = bf16[48,256,256]{2,0,1:T(8,128)(2,1)S(1)} fusion(bf16[16,256,256]{2,0,1:T(8,128)(2,1)} %collective-permute-done.1, bf16[16,256,256]{2,0,1:T(8,128)(2,1)S(1)} %and_select_fusion.1, bf16[16,256,256]{2,0,1:T(8,128)(2,1)} %collective-permute-done), kind=kLoop, calls=%fused_computation.3 | loop fusion | flops 18874368 | bytes 12582912 | tf_op jit(solution)/shard_map/concatenate | solution.py:16
  40.8 4.9 %copy.15 = bf16[48,256,256]{2,1,0:T(8,128)(2,1)} copy(bf16[48,256,256]{2,0,1:T(8,128)(2,1)S(1)} %pad_maximum_fusion) | data formatting | bytes 12582912 | tf_op jit(solution)/shard_map/concatenate | solution.py:16
  45.7 7.7 %gather_fusion = bf16[48,256,256]{2,1,0:T(8,128)(2,1)} fusion(bf16[48,256,256]{2,1,0:T(8,128)(2,1)} %copy.15, s32[1024]{0:T(1024)S(1)} %pad_clamp_fusion), kind=kCustom, calls=%fused_computation | custom fusion | bytes 12583104 | tf_op jit(solution)/shard_map/jit(_take)/gather | solution.py:47
  53.4 11.1 %fusion.2 = f32[48,256,256]{2,1,0:T(8,128)} fusion(bf16[48,1,256,256]{3,2,1,0:T(8,128)(2,1)} %param.10, bf16[48,1,256,256]{3,2,1,0:T(8,128)(2,1)} %param.9, bf16[48,256,256]{2,1,0:T(8,128)(2,1)} %gather_fusion, pred[48]{0:T(512)(128)(4,1)S(1)} %get-tuple-element.5), kind=kOutput, calls=%fused_computation.4 | convolution fusion | flops 3227516928 | bytes 31457328 | tf_op jit(solution)/shard_map/jac,jdc->jad/dot_general | solution.py:51
  64.5 17.9 %fusion.9 = bf16[16,256,256]{2,0,1:T(8,128)(2,1)S(1)} fusion(pred[16,256]{1,0:T(8,128)(4,1)S(1)} %iota_compare_fusion, pred[16,256]{0,1:T(8,128)(4,1)S(1)} %copy.13, f32[48,256,256]{2,1,0:T(8,128)} %fusion.2, f32[48]{0:T(128)S(1)} %compare_convert_fusion, s32[48]{0:T(128)S(1)} %subtract_bitcast_fusion), kind=kOutput, calls=%fused_computation.13 | convolution fusion | flops 607127040 | bytes 14688640 | tf_op jit(solution)/shard_map/js,jad->sad/dot_general | solution.py:57
  82.4 36.2 %all_to_all.5 = bf16[16,16,16,256]{3,1,2,0:T(8,128)(2,1)S(1)} all-to-all(bf16[16,16,16,256]{3,1,2,0:T(8,128)(2,1)S(1)} %bitcast.23), channel_id=1, replica_groups=mesh['sector'=16,'term'=16] {'term'}, dimensions={0} | all-to-all | bytes 4194304 | tf_op jit(solution)/shard_map/all_to_all | solution.py:27
  118.6 0.3 convert_reduce_fusion
  118.9 0.9 copy.19
  (2 shorter events, 0.0 us)
Async XLA Ops:
  7.1 26.2 %collective-permute-start = (bf16[16,256,256]{2,0,1:T(8,128)(2,1)S(1)}, bf16[16,256,256]{2,0,1:T(8,128)(2,1)}, u32[]{:S(2)}, u32[]{:S(2)}) collective-permute-start(bf16[16,256,256]{2,0,1:T(8,128)(2,1)S(1)} %and_select_fusion.1), channel_id=1, source_target_pairs={{0,16},{16,32},{32,48},{48,64},{64,80},{80,96},{96,112},{112,128},... | collective-permute-start | bytes 6291464 | tf_op jit(solution)/shard_map/ppermute | solution.py:14
  10.3 27.5 %collective-permute-start.1 = (bf16[16,256,256]{2,0,1:T(8,128)(2,1)S(1)}, bf16[16,256,256]{2,0,1:T(8,128)(2,1)}, u32[]{:S(2)}, u32[]{:S(2)}) collective-permute-start(bf16[16,256,256]{2,0,1:T(8,128)(2,1)S(1)} %and_select_fusion.1), channel_id=1, source_target_pairs={{16,0},{32,16},{48,32},{64,48},{80,64},{96,80},{112,96},{128,112},... | collective-permute-start | bytes 6291464 | tf_op jit(solution)/shard_map/ppermute | solution.py:15
where the time goes:
time: 120 us
  blocking collectives  36.2 us (30%)
  matrix products  29 us (24%)
  waiting for transfers between devices  23.5 us (20%)
  local copies, waits for them, and re-layouts  13.6 us (11%)
  other arithmetic  11.6 us (10%)
  starting transfers between devices  5.13 us (4%)
    all_to_all x1, blocking collectives, sum_at_owner(): tiles = lax.all_to_all(cut_along(x, dim, devices), axis, 0, 0, tiled=True)  36.2 us
    ppermute x1, waiting for transfers between devices, extended(): before = lax.ppermute(last, axis, up)  19 us
    dot_general x1, matrix products, on_device(): jnp.einsum('js,jad->sad', selector, contribution, precision=lax.Precision...  17.9 us
    dot_general x1, matrix products, on_device(): jnp.einsum('jac,jdc->jad', inner, right, preferred_element_type=jnp.float32)  11.1 us
    gather x1, local copies, waits for them, and re-layouts, on_device(): picked = jnp.take(nearby, local_src, axis=0)  7.7 us
    select_n x1, other arithmetic, on_device(): masked = jnp.where(keep, psi, jnp.zeros_like(psi))  6.21 us
    concatenate x1, local copies, waits for them, and re-layouts, extended(): x = jnp.concatenate([before, x, after], axis=dim)  4.92 us
    ppermute x1, waiting for transfers between devices, extended(): after = lax.ppermute(leading, axis, down)  4.5 us
  transfers between devices with their start and end apart: 2, of which 2 were waited for; matrix products, arithmetic and copies ran while one was open for 1% of the time, Pallas kernels for 0%

commit v1 on v0

v1 whole, which is shorter than its diff:
```python
import jax
import jax.numpy as jnp
from jax import lax
from jax.experimental import pallas as pl
from jax.experimental.pallas import tpu as pltpu
from jax.sharding import PartitionSpec as P


Z, CORES, Y, X = (8, 2, 4, 4)
BLOCK = 256
SECS = 16
SLOTS = 48
NOWHERE = -4096
SHARD = 3
DIRECT = SECS - 4 * SHARD
AXES = ("sector", "term")
HBM = pl.BlockSpec(memory_space=pltpu.HBM)
VMEM = pl.BlockSpec(memory_space=pltpu.VMEM)
SMEM = pl.BlockSpec(memory_space=pltpu.SMEM)
WIDTH = 6
CHUNK = 4
VLIM = 8 * 1024 * 1024


def device(z, core, y, x):
    return (z * CORES + core) * (Y * X) + y * X + x


def every():
    return [
        (z, core, y, x) for z in range(Z) for core in range(CORES) for y in range(Y) for x in range(X)
    ]


def partner_pairs():
    return [(device(z, c, y, x), device(z, 1 - c, y, x)) for z, c, y, x in every()]


def between_chips_pairs():
    return [
        (device(z, c, y, x), device(z + (1 if c else -1), 1 - c, y, x))
        for z, c, y, x in every()
        if 0 <= z + (1 if c else -1) < Z
    ]


def line_pairs(step, first):
    pairs = []
    for z, c, y, x in every():
        along_x = (c == 0) == first
        to = (y, (x + step) % X) if along_x else ((y + step) % Y, x)
        pairs.append((device(z, c, y, x), device(z, c, *to)))
    return pairs


def send(x, pairs):
    return lax.ppermute(x, AXES, pairs)


def place():
    sector = lax.axis_index("sector")
    term = lax.axis_index("term")
    return (sector, sector % CORES, term // X, term % X)


def blocks(n):
    return jax.ShapeDtypeStruct((n, BLOCK, BLOCK), jnp.bfloat16)


def masker():
    row = lax.broadcasted_iota(jnp.int32, (BLOCK, BLOCK), 0)
    col = lax.broadcasted_iota(jnp.int32, (BLOCK, BLOCK), 1)
    most = jnp.maximum(row, col)
    return lambda x, size: jnp.where(most < size, x.astype(jnp.float32), 0.0).astype(jnp.bfloat16)


def near_kernel(sizes_in, psi, near, buf, sizes, sems):
    get_sizes = pltpu.make_async_copy(sizes_in, sizes, sems.at[SHARD])
    get_sizes.start()
    _, core, y, x = place()
    c = jnp.where(core == 0, y, x)
    mask = masker()

    def fetch(i):
        return pltpu.make_async_copy(psi.at[c * SHARD + i], buf.at[i], sems.at[i])

    for i in range(SHARD):
        fetch(i).start()
    get_sizes.wait()
    for i in range(SHARD):
        fetch(i).wait()
        near[i] = mask(buf[i], sizes[c * SHARD + i])


def near_blocks(psi, sizes):
    return pl.pallas_call(
        near_kernel,
        in_specs=[HBM, HBM],
        out_specs=VMEM,
        out_shape=blocks(SHARD),
        scratch_shapes=[
            pltpu.VMEM((SHARD, BLOCK, BLOCK), jnp.bfloat16),
            pltpu.SMEM((SECS,), jnp.int32),
            pltpu.SemaphoreType.DMA((SHARD + 1,)),
        ],
        compiler_params=PARAMS,
        name="near_blocks",
    )(sizes, psi)


def prep_kernel(sizes_in, psi, masked, far, buf, sizes, sems):
    get_sizes = pltpu.make_async_copy(sizes_in, sizes, sems.at[SECS])
    get_sizes.start()
    _, core, y, x = place()
    c2 = (jnp.where(core == 0, y, x) + 2) % 4
    mask = masker()

    def fetch(k):
        return pltpu.make_async_copy(psi.at[k], buf.at[k], sems.at[k])

    for k in range(SECS):
        fetch(k).start()
    get_sizes.wait()

    def one(k, carry):
        fetch(k).wait()
        masked[k] = mask(buf[k], sizes[k])
        return carry

    lax.fori_loop(0, SECS, one, 0)
    for i in range(SHARD):
        far[i] = masked[c2 * SHARD + i]
    for i in range(DIRECT):
        far[SHARD + i] = masked[4 * SHARD + i]


def prep(psi, sizes):
    return pl.pallas_call(
        prep_kernel,
        in_specs=[HBM, HBM],
        out_specs=[VMEM] * 2,
        out_shape=[blocks(SECS), blocks(SHARD + DIRECT)],
        scratch_shapes=[
            pltpu.VMEM((SECS, BLOCK, BLOCK), jnp.bfloat16),
            pltpu.SMEM((SECS,), jnp.int32),
            pltpu.SemaphoreType.DMA((SECS + 1,)),
        ],
        compiler_params=PARAMS,
        name="prep",
    )(sizes, psi)


def listed(order, low, src):
    def collect(j, count):
        at = src[j] - low
        order[count] = j
        return count + ((at >= 0) & (at < SECS)).astype(jnp.int32)

    return lax.fori_loop(0, SLOTS, collect, jnp.int32(0))


def add_listed(order, count, low, tgt, src, lbuf, rbuf, wave, acc, ready):
    base = lax.axis_index("sector") * SECS

    def step(n, state):
        first = n * WIDTH
        state = ready(order[jnp.minimum(first + WIDTH, count) - 1], state)
        for u in range(WIDTH):
            there = first + u < count
            j = jnp.where(there, order[first + u], 0)
            s = jnp.where(there, src[j] - low, 0)
            t = jnp.where(there, tgt[j] - base, SECS)
            inner = jnp.dot(
                lbuf[j], wave[s], preferred_element_type=jnp.float32
            ).astype(jnp.bfloat16)
            acc[t] += lax.dot_general(
                inner, rbuf[j], (((1,), (1,)), ((), ())), preferred_element_type=jnp.float32
            )
        return state

    return lax.fori_loop(0, (count + WIDTH - 1) // WIDTH, step, jnp.int32(0))


def work_kernel(tgt, src, left, right, masked, partner, acc, lbuf, rbuf, lsem, rsem, order):
    sector, core, _, _ = place()


    def fetches(k):
        at = pl.ds(k * CHUNK, CHUNK)
        return (
            pltpu.make_async_copy(left.at[at, 0], lbuf.at[at], lsem.at[k]),
            pltpu.make_async_copy(right.at[at, 0], rbuf.at[at], rsem.at[k]),
        )

    for k in range(SLOTS // CHUNK):
        for copy in fetches(k):
            copy.start()

    own_low = sector * SECS
    partner_low = (sector + 1 - 2 * core) * SECS
    own_count = listed(order.at[0], own_low, src)
    partner_count = listed(order.at[1], partner_low, src)

    def zero(s, carry):
        acc[s] = jnp.zeros((BLOCK, BLOCK), jnp.float32)
        return carry

    lax.fori_loop(0, SECS, zero, 0)

    def wait(k, carry):
        for copy in fetches(k):
            copy.wait()
        return carry

    def ready(j, waited):
        need = jnp.maximum(j // CHUNK + 1, waited)
        lax.fori_loop(waited, need, wait, 0)
        return need

    waited = add_listed(order.at[0], own_count, own_low, tgt, src, lbuf, rbuf, masked, acc, ready)
    lax.fori_loop(waited, SLOTS // CHUNK, wait, 0)
    add_listed(
        order.at[1], partner_count, partner_low, tgt, src, lbuf, rbuf, partner, acc, lambda j, w: w
    )


def halo_kernel(
    tgt, src, sizes, lbuf, rbuf, own, plus, minus, far, before,
    acc, out_own, out_plus, out_minus, out_cross,
    wave, order,
):
    sector, core, y, x = place()
    c = jnp.where(core == 0, x, y)
    for ref, at in ((own, c), (plus, (c + 3) % 4), (minus, (c + 1) % 4), (far, (c + 2) % 4)):
        for i in range(SHARD):
            wave[at * SHARD + i] = ref[i]
    for i in range(DIRECT):
        wave[4 * SHARD + i] = far[SHARD + i]
    low = (sector - 1 + 2 * core) * SECS
    count = listed(order, low, src)
    add_listed(order, count, low, tgt, src, lbuf, rbuf, wave, acc, lambda j, w: w)

    q_rows = jnp.where(core == 0, 64, 16)
    c_rows = jnp.where(core == 0, 16, 64)
    row = lax.broadcasted_iota(jnp.int32, (16, BLOCK), 0)
    col = lax.broadcasted_iota(jnp.int32, (16, BLOCK), 1)

    def put(s, carry):
        size = sizes[s]
        for step, out in ((1, out_plus), (3, out_minus), (2, out_cross), (0, out_own)):
            to = (c + step) % 4
            for q in range(4):
                at = pl.multiple_of(q * q_rows + to * c_rows, 16)
                piece = acc[s, pl.ds(at, 16), :]
                kept = jnp.maximum(row + at, col) < size
                out[s, q] = jnp.where(kept, piece, 0.0).astype(jnp.bfloat16)
        return carry

    lax.fori_loop(0, SECS, put, 0)


def merge_kernel(own, plus, minus, cross, mine, to_plus, to_minus, to_cross):
    _, core, y, x = place()
    c = jnp.where(core == 0, y, x)

    def put(s, carry):
        for step, out in ((1, to_plus), (3, to_minus), (2, to_cross), (0, mine)):
            at = (c + step) % 4
            pieces = [ref[s, at].astype(jnp.float32) for ref in (own, plus, minus, cross)]
            out[s] = (pieces[0] + pieces[1] + (pieces[2] + pieces[3])).astype(out.dtype)
        return carry

    lax.fori_loop(0, SECS, put, 0)


def merge(*pieces):
    message = jax.ShapeDtypeStruct((SECS, 16, BLOCK), jnp.bfloat16)
    return pl.pallas_call(
        merge_kernel,
        in_specs=[VMEM] * 4,
        out_specs=[VMEM] * 4,
        out_shape=[jax.ShapeDtypeStruct((SECS, 16, BLOCK), jnp.float32)] + [message] * 3,
        compiler_params=PARAMS,
        name="merge",
    )(*pieces)


def last_kernel(mine, plus, minus, cross, out):
    pieces = [ref[...].astype(jnp.float32) for ref in (mine, plus, minus, cross)]
    out[...] = pieces[0] + pieces[1] + (pieces[2] + pieces[3])


def last_sum(*pieces):
    return pl.pallas_call(
        last_kernel,
        in_specs=[VMEM] * 4,
        out_specs=VMEM,
        out_shape=jax.ShapeDtypeStruct((SECS, 16, BLOCK), jnp.float32),
        compiler_params=PARAMS,
        name="last_sum",
    )(*pieces)


ACC = jax.ShapeDtypeStruct((SECS + 1, BLOCK, BLOCK), jnp.float32)
COST = pl.CostEstimate(flops=2 * 16 * 2 * BLOCK**3, bytes_accessed=16 * 4 * BLOCK * BLOCK, transcendentals=0)
PARAMS = pltpu.CompilerParams(vmem_limit_bytes=VLIM)


def work_slots(tgt, src, left, right, masked, partner):
    chunks = SLOTS // CHUNK
    return pl.pallas_call(
        work_kernel,
        in_specs=[SMEM] * 2 + [HBM] * 2 + [VMEM] * 2,
        out_specs=[VMEM] * 3,
        out_shape=[ACC, blocks(SLOTS), blocks(SLOTS)],
        scratch_shapes=[
            pltpu.SemaphoreType.DMA((chunks,)),
            pltpu.SemaphoreType.DMA((chunks,)),
            pltpu.SMEM((2, SLOTS + WIDTH), jnp.int32),
        ],
        compiler_params=PARAMS,
        cost_estimate=COST,
        name="work_slots",
    )(tgt, src, left, right, masked, partner)


def halo_slots(tgt, src, sizes, left, right, own, plus, minus, far, before):
    message = jax.ShapeDtypeStruct((SECS, 4, 16, BLOCK), jnp.bfloat16)
    return pl.pallas_call(
        halo_kernel,
        in_specs=[SMEM] * 3 + [VMEM] * 7,
        out_specs=[VMEM] * 5,
        out_shape=[ACC] + [message] * 4,
        scratch_shapes=[
            pltpu.VMEM((SECS, BLOCK, BLOCK), jnp.bfloat16),
            pltpu.SMEM((SLOTS + WIDTH,), jnp.int32),
        ],
        input_output_aliases={9: 0},
        compiler_params=PARAMS,
        cost_estimate=COST,
        name="halo_slots",
    )(tgt, src, sizes, left, right, own, plus, minus, far, before)


def on_device(psi, sector_sizes, left_env, right_env, target, source, live_count):
    target = target.reshape(SLOTS)
    alive = jnp.arange(SLOTS, dtype=jnp.int32) < live_count.reshape(1)
    source = jnp.where(alive, source.reshape(SLOTS), NOWHERE)
    left_env, right_env, psi, sizes = [
        pltpu.with_memory_space_constraint(v, pltpu.HBM)
        for v in (left_env, right_env, psi, sector_sizes)
    ]
    near = near_blocks(psi, sizes)
    near, psi = lax.optimization_barrier((near, psi))
    h_near = send(near, between_chips_pairs())
    masked, far = prep(psi, sizes)
    h_far = send(far, between_chips_pairs())
    from_partner = send(masked, partner_pairs())
    h_plus = send(h_near, line_pairs(1, True))
    h_minus = send(h_near, line_pairs(-1, True))
    total, left, right = work_slots(
        target, source, left_env, right_env, masked, from_partner
    )
    _, m_own, m_plus, m_minus, m_cross = halo_slots(
        target, source, sector_sizes, left, right,
        h_near, h_plus, h_minus, h_far, total,
    )
    g_cross = send(m_cross, line_pairs(2, True))
    g_plus = send(m_plus, line_pairs(1, True))
    g_minus = send(m_minus, line_pairs(-1, True))
    mine, s_plus, s_minus, s_cross = merge(m_own, g_plus, g_minus, g_cross)
    t_cross = send(s_cross, line_pairs(2, False))
    t_plus = send(s_plus, line_pairs(1, False))
    t_minus = send(s_minus, line_pairs(-1, False))
    return last_sum(mine, t_plus, t_minus, t_cross)


def solution(mesh):
    placed = (
        P("sector", None, None),
        P("sector"),
        P("term", "sector", None, None),
        P("term", "sector", None, None),
        P("term", "sector"),
        P("term", "sector"),
        P("term", "sector"),
    )
    return jax.shard_map(
        on_device, mesh=mesh, in_specs=placed, out_specs=P("sector", "term", None), check_vma=False
    )
```

time: 120 us -> 66.4 us (0.55)
  the two profiles are of different devices: /device:TPU:161 before, /device:TPU:224 now
where the time goes in v1:
time: 66.4 us; the launch traced here: 66.2 us
  waiting for transfers between devices  34.8 us (52%)
  starting transfers between devices  17.8 us (27%)
  Pallas kernels  12.8 us (19%)
  between operations  0.77 us (1%)
    ppermute x11, waiting for transfers between devices, send(): return lax.ppermute(x, AXES, pairs)  34.8 us
    ppermute x11, starting transfers between devices, send(): return lax.ppermute(x, AXES, pairs)  17.8 us
    pallas_call x1, Pallas kernels, work_slots(): pl.pallas_call(work_kernel, in_specs=[SMEM] * 2 + [HBM] * 2 + [VMEM] * 2,...  6.02 us
    pallas_call x1, Pallas kernels, halo_slots(): pl.pallas_call(halo_kernel, in_specs=[SMEM] * 3 + [VMEM] * 7, out_specs=[...  2.59 us
    pallas_call x1, Pallas kernels, prep(): pl.pallas_call(prep_kernel, in_specs=[HBM, HBM], out_specs=[VMEM] * 2, ou...  1.85 us
  transfers between devices with their start and end apart: 11, of which 8 were waited for; matrix products, arithmetic and copies ran while one was open for 0% of the time, Pallas kernels for 9%

profile of v1, /device:TPU:224, one launch (start us, length us, event | category | flops | bytes accessed | tf_op | source)
XLA Modules:
  0.0 66.2 jit_solution(4778841867744939235)
XLA Ops:
  0.0 0.0 copy-start.2
  0.0 0.0 copy-start.1
  0.0 1.1 %near_blocks.1 = bf16[3,256,256]{2,1,0:T(8,128)(2,1)S(1)} custom-call(s32[16]{0:T(128)} %sizes.1, bf16[16,256,256]{2,1,0:T(8,128)(2,1)} %psi.2), custom_call_target="tpu_custom_call" | custom-call | tf_op jit(solution)/shard_map/near_blocks/pallas_call | solution.py:96
  1.1 1.8 %prep.1 = (bf16[16,256,256]{2,1,0:T(8,128)(2,1)S(1)}, bf16[7,256,256]{2,1,0:T(8,128)(2,1)S(1)}) custom-call(s32[16]{0:T(128)} %sizes.1, bf16[16,256,256]{2,1,0:T(8,128)(2,1)} %psi.2), custom_call_target="tpu_custom_call" | custom-call | tf_op jit(solution)/shard_map/prep/pallas_call | solution.py:138
  3.0 0.1 collective-permute-start
  3.1 3.0 %collective-permute-start.4 = (bf16[7,256,256]{2,1,0:T(8,128)(2,1)S(1)}, bf16[7,256,256]{2,1,0:T(8,128)(2,1)S(1)}, u32[]{:S(2)}, u32[]{:S(2)}) collective-permute-start(bf16[7,256,256]{2,1,0:T(8,128)(2,1)S(1)} %get-tuple-element.25), channel_id=1, source_target_pairs={{16,32},{17,33},{18,34},{19,35},{20,36},{21,37},{22,38},{23,39},{2... | collective-permute-start | bytes 2752520 | tf_op jit(solution)/shard_map/ppermute | solution.py:57
  6.1 2.6 %collective-permute-start.1 = (bf16[3,256,256]{2,1,0:T(8,128)(2,1)S(1)}, bf16[3,256,256]{2,1,0:T(8,128)(2,1)S(1)}, u32[]{:S(2)}, u32[]{:S(2)}) collective-permute-start(bf16[3,256,256]{2,1,0:T(8,128)(2,1)S(1)} %near_blocks.1), channel_id=1, source_target_pairs={{16,32},{17,33},{18,34},{19,35},{20,36},{21,37},{22,38},{23,39},{2... | collective-permute-start | bytes 1179656 | tf_op jit(solution)/shard_map/ppermute | solution.py:57
  8.7 13.3 %collective-permute-done.1.own = bf16[3,256,256]{2,1,0:T(8,128)(2,1)S(1)} collective-permute-done((bf16[3,256,256]{2,1,0:T(8,128)(2,1)S(1)}, bf16[3,256,256]{2,1,0:T(8,128)(2,1)S(1)}, u32[]{:S(2)}, u32[]{:S(2)}) %collective-permute-start.1) | collective-permute-done | bytes 393248 | tf_op jit(solution)/shard_map/ppermute | solution.py:57
  22.0 2.8 %collective-permute-start.3 = (bf16[3,256,256]{2,1,0:T(8,128)(2,1)S(1)}, bf16[3,256,256]{2,1,0:T(8,128)(2,1)S(1)}, u32[]{:S(2)}, u32[]{:S(2)}) collective-permute-start(bf16[3,256,256]{2,1,0:T(8,128)(2,1)S(1)} %collective-permute-done.1.own), channel_id=1, source_target_pairs={{0,3},{1,0},{2,1},{3,2},{4,7},{5,4},{6,5},{7,6},{8,11},{9,8},{10,9... | collective-permute-start | bytes 1179656 | tf_op jit(solution)/shard_map/ppermute | solution.py:57
  24.8 0.0 collective-permute-start.2
  25.4 0.0 copy-done.2
  25.5 0.0 collective-permute-done.partner
  25.5 0.0 copy-done.1
  25.5 0.0 copy-start
  25.5 6.0 %work_slots.1 = (f32[17,256,256]{2,1,0:T(8,128)S(1)}, bf16[48,256,256]{2,1,0:T(8,128)(2,1)S(1)}, bf16[48,256,256]{2,1,0:T(8,128)(2,1)S(1)}) custom-call(s32[48]{0:T(128)S(1)} %bitcast.5, s32[48]{0:T(128)S(1)} %compare_select_fusion.src, bf16[48,1,256,256]{3,2,1,0:T(8,128)(2,1)} %left.1, bf16[48,1,256,256]{3,2,1,0:T(8,128)(2,1)} %right.1, ...), custom_call_target="tpu_custom_call" | custom-call | flops 1073741824 | bytes 4194304 | tf_op jit(solution)/shard_map/work_slots/pallas_call | solution.py:311
  31.5 0.0 collective-permute-done.3.minus
  31.5 2.2 %collective-permute-done.2.plus = bf16[3,256,256]{2,1,0:T(8,128)(2,1)S(1)} collective-permute-done((bf16[3,256,256]{2,1,0:T(8,128)(2,1)S(1)}, bf16[3,256,256]{2,1,0:T(8,128)(2,1)S(1)}, u32[]{:S(2)}, u32[]{:S(2)}) %collective-permute-start.2) | collective-permute-done | bytes 393248 | tf_op jit(solution)/shard_map/ppermute | solution.py:57
  33.8 0.0 collective-permute-done.4.far
  33.8 0.0 copy-done
  33.8 2.6 %halo_slots.1 = (f32[17,256,256]{2,1,0:T(8,128)S(1)}, bf16[16,4,16,256]{3,2,1,0:T(8,128)(2,1)S(1)}, bf16[16,4,16,256]{3,2,1,0:T(8,128)(2,1)S(1)}, bf16[16,4,16,2...) custom-call(s32[48]{0:T(128)S(1)} %bitcast.6, s32[48]{0:T(128)S(1)} %compare_select_fusion.src, ...), custom_call_target="tpu_custom_call", output_to_operand_aliasing={{0}: (9, {})} | custom-call | flops 1073741824 | bytes 4194304 | tf_op jit(solution)/shard_map/halo_slots/pallas_call | solution.py:329
  36.4 0.5 collective-permute-start.5
  36.9 4.1 %collective-permute-start.6 = (bf16[16,4,16,256]{3,2,1,0:T(8,128)(2,1)S(1)}, bf16[16,4,16,256]{3,2,1,0:T(8,128)(2,1)S(1)}, u32[]{:S(2)}, u32[]{:S(2)}) collective-permute-start(bf16[16,4,16,256]{3,2,1,0:T(8,128)(2,1)S(1)} %get-tuple-element.29), channel_id=1, source_target_pairs={{0,3},{1,0},{2,1},{3,2},{4,7},{5,4},{6,5},{7,6},{8,11},{9,8},{10,9... | collective-permute-start | bytes 1572872 | tf_op jit(solution)/shard_map/ppermute | solution.py:57
  41.0 1.4 %collective-permute-start.7 = (bf16[16,4,16,256]{3,2,1,0:T(8,128)(2,1)S(1)}, bf16[16,4,16,256]{3,2,1,0:T(8,128)(2,1)S(1)}, u32[]{:S(2)}, u32[]{:S(2)}) collective-permute-start(bf16[16,4,16,256]{3,2,1,0:T(8,128)(2,1)S(1)} %get-tuple-element.30), channel_id=1, source_target_pairs={{0,2},{1,3},{2,0},{3,1},{4,6},{5,7},{6,4},{7,5},{8,10},{9,11},{10,... | collective-permute-start | bytes 1572872 | tf_op jit(solution)/shard_map/ppermute | solution.py:57
  42.4 5.7 %collective-permute-done.5.plus = bf16[16,4,16,256]{3,2,1,0:T(8,128)(2,1)S(1)} collective-permute-done((bf16[16,4,16,256]{3,2,1,0:T(8,128)(2,1)S(1)}, bf16[16,4,16,256]{3,2,1,0:T(8,128)(2,1)S(1)}, u32[]{:S(2)}, u32[]{:S(2)}) %collective-permute-start.5) | collective-permute-done | bytes 524320 | tf_op jit(solution)/shard_map/ppermute | solution.py:57
  48.1 5.2 %collective-permute-done.6.minus = bf16[16,4,16,256]{3,2,1,0:T(8,128)(2,1)S(1)} collective-permute-done((bf16[16,4,16,256]{3,2,1,0:T(8,128)(2,1)S(1)}, bf16[16,4,16,256]{3,2,1,0:T(8,128)(2,1)S(1)}, u32[]{:S(2)}, u32[]{:S(2)}) %collective-permute-start.6) | collective-permute-done | bytes 524320 | tf_op jit(solution)/shard_map/ppermute | solution.py:57
  53.4 1.8 %collective-permute-done.7.cross = bf16[16,4,16,256]{3,2,1,0:T(8,128)(2,1)S(1)} collective-permute-done((bf16[16,4,16,256]{3,2,1,0:T(8,128)(2,1)S(1)}, bf16[16,4,16,256]{3,2,1,0:T(8,128)(2,1)S(1)}, u32[]{:S(2)}, u32[]{:S(2)}) %collective-permute-start.7) | collective-permute-done | bytes 524320 | tf_op jit(solution)/shard_map/ppermute | solution.py:57
  55.2 0.4 merge.1
  55.6 0.8 %collective-permute-start.8 = (bf16[16,16,256]{2,1,0:T(8,128)(2,1)S(1)}, bf16[16,16,256]{2,1,0:T(8,128)(2,1)S(1)}, u32[]{:S(2)}, u32[]{:S(2)}) collective-permute-start(bf16[16,16,256]{2,1,0:T(8,128)(2,1)S(1)} %get-tuple-element.32), channel_id=1, source_target_pairs={{0,4},{1,5},{2,6},{3,7},{4,8},{5,9},{6,10},{7,11},{8,12},{9,13},{1... | collective-permute-start | bytes 393224 | tf_op jit(solution)/shard_map/ppermute | solution.py:57
  56.4 2.5 %collective-permute-start.9 = (bf16[16,16,256]{2,1,0:T(8,128)(2,1)S(1)}, bf16[16,16,256]{2,1,0:T(8,128)(2,1)S(1)}, u32[]{:S(2)}, u32[]{:S(2)}) collective-permute-start(bf16[16,16,256]{2,1,0:T(8,128)(2,1)S(1)} %get-tuple-element.33), channel_id=1, source_target_pairs={{0,12},{1,13},{2,14},{3,15},{4,0},{5,1},{6,2},{7,3},{8,4},{9,5},{1... | collective-permute-start | bytes 393224 | tf_op jit(solution)/shard_map/ppermute | solution.py:57
  58.9 0.0 collective-permute-start.10
  58.9 2.9 %collective-permute-done.8.plus = bf16[16,16,256]{2,1,0:T(8,128)(2,1)S(1)} collective-permute-done((bf16[16,16,256]{2,1,0:T(8,128)(2,1)S(1)}, bf16[16,16,256]{2,1,0:T(8,128)(2,1)S(1)}, u32[]{:S(2)}, u32[]{:S(2)}) %collective-permute-start.8) | collective-permute-done | bytes 131104 | tf_op jit(solution)/shard_map/ppermute | solution.py:57
  61.9 1.0 %collective-permute-done.9.minus = bf16[16,16,256]{2,1,0:T(8,128)(2,1)S(1)} collective-permute-done((bf16[16,16,256]{2,1,0:T(8,128)(2,1)S(1)}, bf16[16,16,256]{2,1,0:T(8,128)(2,1)S(1)}, u32[]{:S(2)}, u32[]{:S(2)}) %collective-permute-start.9) | collective-permute-done | bytes 131104 | tf_op jit(solution)/shard_map/ppermute | solution.py:57
  62.9 2.5 %collective-permute-done.10.cross = bf16[16,16,256]{2,1,0:T(8,128)(2,1)S(1)} collective-permute-done((bf16[16,16,256]{2,1,0:T(8,128)(2,1)S(1)}, bf16[16,16,256]{2,1,0:T(8,128)(2,1)S(1)}, u32[]{:S(2)}, u32[]{:S(2)}) %collective-permute-start.10) | collective-permute-done | bytes 131104 | tf_op jit(solution)/shard_map/ppermute | solution.py:57
  65.4 0.8 %last_sum.1 = f32[16,16,256]{2,1,0:T(8,128)} custom-call(f32[16,16,256]{2,1,0:T(8,128)S(1)} %get-tuple-element.31.mine, bf16[16,16,256]{2,1,0:T(8,128)(2,1)S(1)} %collective-permute-done.8.plus, bf16[16,16,256]{2,1,0:T(8,128)(2,1)S(1)} %collective-permute-done.9.minus, bf16[16,16,256]{2,1,0:T(8,128)(2,1)S(1)} %collective-permute-done.10.cross), custom_call_target="tpu_custom_call" | custom-call | tf_op jit(solution)/shard_map/last_sum/pallas_call | solution.py:294
  (1 shorter events, 0.0 us)
Async XLA Ops:
  0.0 25.4 %copy-start.2 = (s32[48,1]{0,1:T(1,128)S(1)}, s32[48,1]{0,1:T(1,128)}, u32[]{:S(2)}) copy-start(s32[48,1]{0,1:T(1,128)} %param.12) | copy-start | bytes 580
  0.0 25.5 %copy-start.1 = (s32[48,1]{0,1:T(1,128)S(1)}, s32[48,1]{0,1:T(1,128)}, u32[]{:S(2)}) copy-start(s32[48,1]{0,1:T(1,128)} %param.11) | copy-start | bytes 580
  3.0 22.5 %collective-permute-start = (bf16[16,256,256]{2,1,0:T(8,128)(2,1)S(1)}, bf16[16,256,256]{2,1,0:T(8,128)(2,1)S(1)}, u32[]{:S(2)}, u32[]{:S(2)}) collective-permute-start(bf16[16,256,256]{2,1,0:T(8,128)(2,1)S(1)} %get-tuple-element.21.masked), channel_id=1, source_target_pairs={{0,16},{1,17},{2,18},{3,19},{4,20},{5,21},{6,22},{7,23},{8,24},{9,... | collective-permute-start | bytes 6291464 | tf_op jit(solution)/shard_map/ppermute | solution.py:57
  3.1 30.7 %collective-permute-start.4 = (bf16[7,256,256]{2,1,0:T(8,128)(2,1)S(1)}, bf16[7,256,256]{2,1,0:T(8,128)(2,1)S(1)}, u32[]{:S(2)}, u32[]{:S(2)}) collective-permute-start(bf16[7,256,256]{2,1,0:T(8,128)(2,1)S(1)} %get-tuple-element.25), channel_id=1, source_target_pairs={{16,32},{17,33},{18,34},{19,35},{20,36},{21,37},{22,38},{23,39},{2... | collective-permute-start | bytes 2752520 | tf_op jit(solution)/shard_map/ppermute | solution.py:57
  6.1 15.9 %collective-permute-start.1 = (bf16[3,256,256]{2,1,0:T(8,128)(2,1)S(1)}, bf16[3,256,256]{2,1,0:T(8,128)(2,1)S(1)}, u32[]{:S(2)}, u32[]{:S(2)}) collective-permute-start(bf16[3,256,256]{2,1,0:T(8,128)(2,1)S(1)} %near_blocks.1), channel_id=1, source_target_pairs={{16,32},{17,33},{18,34},{19,35},{20,36},{21,37},{22,38},{23,39},{2... | collective-permute-start | bytes 1179656 | tf_op jit(solution)/shard_map/ppermute | solution.py:57
  22.0 9.5 %collective-permute-start.3 = (bf16[3,256,256]{2,1,0:T(8,128)(2,1)S(1)}, bf16[3,256,256]{2,1,0:T(8,128)(2,1)S(1)}, u32[]{:S(2)}, u32[]{:S(2)}) collective-permute-start(bf16[3,256,256]{2,1,0:T(8,128)(2,1)S(1)} %collective-permute-done.1.own), channel_id=1, source_target_pairs={{0,3},{1,0},{2,1},{3,2},{4,7},{5,4},{6,5},{7,6},{8,11},{9,8},{10,9... | collective-permute-start | bytes 1179656 | tf_op jit(solution)/shard_map/ppermute | solution.py:57
  24.8 9.0 %collective-permute-start.2 = (bf16[3,256,256]{2,1,0:T(8,128)(2,1)S(1)}, bf16[3,256,256]{2,1,0:T(8,128)(2,1)S(1)}, u32[]{:S(2)}, u32[]{:S(2)}) collective-permute-start(bf16[3,256,256]{2,1,0:T(8,128)(2,1)S(1)} %collective-permute-done.1.own), channel_id=1, source_target_pairs={{0,1},{1,2},{2,3},{3,0},{4,5},{5,6},{6,7},{7,4},{8,9},{9,10},{10,1... | collective-permute-start | bytes 1179656 | tf_op jit(solution)/shard_map/ppermute | solution.py:57
  25.5 8.3 %copy-start = (s32[16]{0:T(128)S(1)}, s32[16]{0:T(128)}, u32[]{:S(2)}) copy-start(s32[16]{0:T(128)} %sizes.1) | copy-start | bytes 196
  36.4 11.8 %collective-permute-start.5 = (bf16[16,4,16,256]{3,2,1,0:T(8,128)(2,1)S(1)}, bf16[16,4,16,256]{3,2,1,0:T(8,128)(2,1)S(1)}, u32[]{:S(2)}, u32[]{:S(2)}) collective-permute-start(bf16[16,4,16,256]{3,2,1,0:T(8,128)(2,1)S(1)} %get-tuple-element.28), channel_id=1, source_target_pairs={{0,1},{1,2},{2,3},{3,0},{4,5},{5,6},{6,7},{7,4},{8,9},{9,10},{10,1... | collective-permute-start | bytes 1572872 | tf_op jit(solution)/shard_map/ppermute | solution.py:57
  36.9 16.5 %collective-permute-start.6 = (bf16[16,4,16,256]{3,2,1,0:T(8,128)(2,1)S(1)}, bf16[16,4,16,256]{3,2,1,0:T(8,128)(2,1)S(1)}, u32[]{:S(2)}, u32[]{:S(2)}) collective-permute-start(bf16[16,4,16,256]{3,2,1,0:T(8,128)(2,1)S(1)} %get-tuple-element.29), channel_id=1, source_target_pairs={{0,3},{1,0},{2,1},{3,2},{4,7},{5,4},{6,5},{7,6},{8,11},{9,8},{10,9... | collective-permute-start | bytes 1572872 | tf_op jit(solution)/shard_map/ppermute | solution.py:57
  41.0 14.1 %collective-permute-start.7 = (bf16[16,4,16,256]{3,2,1,0:T(8,128)(2,1)S(1)}, bf16[16,4,16,256]{3,2,1,0:T(8,128)(2,1)S(1)}, u32[]{:S(2)}, u32[]{:S(2)}) collective-permute-start(bf16[16,4,16,256]{3,2,1,0:T(8,128)(2,1)S(1)} %get-tuple-element.30), channel_id=1, source_target_pairs={{0,2},{1,3},{2,0},{3,1},{4,6},{5,7},{6,4},{7,5},{8,10},{9,11},{10,... | collective-permute-start | bytes 1572872 | tf_op jit(solution)/shard_map/ppermute | solution.py:57
  55.6 6.3 %collective-permute-start.8 = (bf16[16,16,256]{2,1,0:T(8,128)(2,1)S(1)}, bf16[16,16,256]{2,1,0:T(8,128)(2,1)S(1)}, u32[]{:S(2)}, u32[]{:S(2)}) collective-permute-start(bf16[16,16,256]{2,1,0:T(8,128)(2,1)S(1)} %get-tuple-element.32), channel_id=1, source_target_pairs={{0,4},{1,5},{2,6},{3,7},{4,8},{5,9},{6,10},{7,11},{8,12},{9,13},{1... | collective-permute-start | bytes 393224 | tf_op jit(solution)/shard_map/ppermute | solution.py:57
  56.4 6.5 %collective-permute-start.9 = (bf16[16,16,256]{2,1,0:T(8,128)(2,1)S(1)}, bf16[16,16,256]{2,1,0:T(8,128)(2,1)S(1)}, u32[]{:S(2)}, u32[]{:S(2)}) collective-permute-start(bf16[16,16,256]{2,1,0:T(8,128)(2,1)S(1)} %get-tuple-element.33), channel_id=1, source_target_pairs={{0,12},{1,13},{2,14},{3,15},{4,0},{5,1},{6,2},{7,3},{8,4},{9,5},{1... | collective-permute-start | bytes 393224 | tf_op jit(solution)/shard_map/ppermute | solution.py:57
  58.9 6.5 %collective-permute-start.10 = (bf16[16,16,256]{2,1,0:T(8,128)(2,1)S(1)}, bf16[16,16,256]{2,1,0:T(8,128)(2,1)S(1)}, u32[]{:S(2)}, u32[]{:S(2)}) collective-permute-start(bf16[16,16,256]{2,1,0:T(8,128)(2,1)S(1)} %get-tuple-element.34), channel_id=1, source_target_pairs={{0,8},{1,9},{2,10},{3,11},{4,12},{5,13},{6,14},{7,15},{8,0},{9,1},... | collective-permute-start | bytes 393224 | tf_op jit(solution)/shard_map/ppermute | solution.py:57

commit v2 on v1

v2 whole, which is shorter than its diff:
```python
import jax
import jax.numpy as jnp
from jax import lax
from jax.experimental import pallas as pl
from jax.experimental.pallas import tpu as pltpu
from jax.sharding import PartitionSpec as P


Z, CORES, Y, X = (8, 2, 4, 4)
BLOCK = 256
SECS = 16
SLOTS = 48
SHARD = 3
DIRECT = SECS - 4 * SHARD
AXES = ("sector", "term")
HBM = pl.BlockSpec(memory_space=pltpu.HBM)
VMEM = pl.BlockSpec(memory_space=pltpu.VMEM)
SMEM = pl.BlockSpec(memory_space=pltpu.SMEM)
WIDTH = 8
HALO_WIDTH = 10
CHUNK = 4
VLIM = 7 * 1024 * 1024


def device(z, core, y, x):
    return (z * CORES + core) * (Y * X) + y * X + x


def every():
    return [
        (z, core, y, x) for z in range(Z) for core in range(CORES) for y in range(Y) for x in range(X)
    ]


def partner_pairs():
    return [(device(z, c, y, x), device(z, 1 - c, y, x)) for z, c, y, x in every()]


def between_chips_pairs():
    return [
        (device(z, c, y, x), device(z + (1 if c else -1), 1 - c, y, x))
        for z, c, y, x in every()
        if 0 <= z + (1 if c else -1) < Z
    ]


def line_pairs(step, first):
    pairs = []
    for z, c, y, x in every():
        along_x = (c == 0) == first
        to = (y, x ^ step) if along_x else (y ^ step, x)
        pairs.append((device(z, c, y, x), device(z, c, *to)))
    return pairs


def send(x, pairs):
    return lax.ppermute(x, AXES, pairs)


def place():
    sector = lax.axis_index("sector")
    term = lax.axis_index("term")
    return (sector, sector % CORES, term // X, term % X)


def blocks(n):
    return jax.ShapeDtypeStruct((n, BLOCK, BLOCK), jnp.bfloat16)


def masker():
    row = lax.broadcasted_iota(jnp.int32, (BLOCK, BLOCK), 0)
    col = lax.broadcasted_iota(jnp.int32, (BLOCK, BLOCK), 1)
    most = jnp.maximum(row, col)
    return lambda x, size: jnp.where(most < size, x.astype(jnp.float32), 0.0).astype(jnp.bfloat16)


def mask_all(sizes_in, psi, near, masked, far, buf, sizes, sems):
    get_sizes = pltpu.make_async_copy(sizes_in, sizes, sems.at[SECS])
    get_sizes.start()
    _, core, y, x = place()
    c = jnp.where(core == 0, y, x)
    c2 = c ^ 2
    mask = masker()

    def fetch(k):
        return pltpu.make_async_copy(psi.at[k], buf.at[k], sems.at[k])

    for k in range(SECS):
        fetch(k).start()
    get_sizes.wait()

    def one(k, carry):
        fetch(k).wait()
        masked[k] = mask(buf[k], sizes[k])
        return carry

    lax.fori_loop(0, SECS, one, 0)
    for i in range(SHARD):
        if near is not None:
            near[i] = masked[c * SHARD + i]
        far[i] = masked[c2 * SHARD + i]
    for i in range(DIRECT):
        far[SHARD + i] = masked[4 * SHARD + i]


def near_kernel(sizes_in, psi, near, masked, far, buf, sizes, sems):
    _, core, y, _ = place()

    @pl.when(core == 1)
    def _():
        mask_all(sizes_in, psi, near, masked, far, buf, sizes, sems)

    @pl.when(core == 0)
    def _():
        get_sizes = pltpu.make_async_copy(sizes_in, sizes, sems.at[SHARD])
        get_sizes.start()
        mask = masker()

        def fetch(i):
            return pltpu.make_async_copy(psi.at[y * SHARD + i], buf.at[i], sems.at[i])

        for i in range(SHARD):
            fetch(i).start()
        get_sizes.wait()
        for i in range(SHARD):
            fetch(i).wait()
            near[i] = mask(buf[i], sizes[y * SHARD + i])


def prep_kernel(sizes_in, psi, masked_in, far_in, masked, far, buf, sizes, sems):
    _, core, _, _ = place()

    @pl.when(core == 0)
    def _():
        mask_all(sizes_in, psi, None, masked, far, buf, sizes, sems)


def mask_scratch():
    return [
        pltpu.VMEM((SECS, BLOCK, BLOCK), jnp.bfloat16),
        pltpu.SMEM((SECS,), jnp.int32),
        pltpu.SemaphoreType.DMA((SECS + 1,)),
    ]


def near_blocks(psi, sizes):
    return pl.pallas_call(
        near_kernel,
        in_specs=[HBM] * 2,
        out_specs=[VMEM] * 3,
        out_shape=[blocks(SHARD), blocks(SECS), blocks(SHARD + DIRECT)],
        scratch_shapes=mask_scratch(),
        compiler_params=PARAMS,
        name="near_blocks",
    )(sizes, psi)


def prep(psi, sizes, masked, far):
    return pl.pallas_call(
        prep_kernel,
        in_specs=[HBM] * 2 + [VMEM] * 2,
        out_specs=[VMEM] * 2,
        out_shape=[blocks(SECS), blocks(SHARD + DIRECT)],
        scratch_shapes=mask_scratch(),
        input_output_aliases={2: 0, 3: 1},
        compiler_params=PARAMS,
        name="prep",
    )(sizes, psi, masked, far)


def listed(order, low, span, src, alive):
    def collect(j, count):
        at = src[j] - low
        order[count] = j
        return count + ((j < alive) & (at >= 0) & (at < span)).astype(jnp.int32)

    return lax.fori_loop(0, SLOTS, collect, jnp.int32(0), unroll=8)


def add_listed(width, order, count, low, tgt, src, lbuf, rbuf, wave, acc, ready):
    base = lax.axis_index("sector") * SECS

    def step(n, state):
        first = n * width
        state = ready(order[jnp.minimum(first + width, count) - 1], state)
        for u in range(width):
            there = first + u < count
            j = jnp.where(there, order[first + u], 0)
            s = jnp.where(there, src[j] - low, 0)
            t = jnp.where(there, tgt[j] - base, SECS)
            inner = jnp.dot(
                lbuf[j], wave[s], preferred_element_type=jnp.float32
            ).astype(jnp.bfloat16)
            acc[t] += lax.dot_general(
                inner, rbuf[j], (((1,), (1,)), ((), ())), preferred_element_type=jnp.float32
            )
        return state

    return lax.fori_loop(0, (count + width - 1) // width, step, jnp.int32(0))


def work_kernel(tgt, src, live, left, right, masked, partner, acc, lbuf, rbuf, wave, order, lsem, rsem):
    def fetches(k):
        at = pl.ds(k * CHUNK, CHUNK)
        return (
            pltpu.make_async_copy(left.at[at, 0], lbuf.at[at], lsem.at[k]),
            pltpu.make_async_copy(right.at[at, 0], rbuf.at[at], rsem.at[k]),
        )

    for k in range(SLOTS // CHUNK):
        for copy in fetches(k):
            copy.start()
    sector, core, _, _ = place()
    low = (sector - core) * SECS

    def fill(s, carry):
        acc[s] = jnp.zeros((BLOCK, BLOCK), jnp.float32)
        wave[core * SECS + s] = masked[s]
        wave[(1 - core) * SECS + s] = partner[s]
        return carry

    lax.fori_loop(0, SECS, fill, 0)
    count = listed(order, low, 2 * SECS, src, live[0, 0])

    def wait(k, carry):
        for copy in fetches(k):
            copy.wait()
        return carry

    def ready(j, waited):
        need = jnp.maximum(j // CHUNK + 1, waited)
        lax.fori_loop(waited, need, wait, 0)
        return need

    waited = add_listed(WIDTH, order, count, low, tgt, src, lbuf, rbuf, wave, acc, ready)
    lax.fori_loop(waited, SLOTS // CHUNK, wait, 0)


def halo_kernel(
    tgt, src, live, sizes, lbuf, rbuf, own, plus, minus, far, before,
    acc, out_own, out_plus, out_minus, out_cross,
    wave, order,
):
    sector, core, y, x = place()
    c = jnp.where(core == 0, x, y)
    for ref, at in ((own, c), (plus, c ^ 1), (minus, c ^ 3), (far, c ^ 2)):
        for i in range(SHARD):
            wave[at * SHARD + i] = ref[i]
    for i in range(DIRECT):
        wave[4 * SHARD + i] = far[SHARD + i]
    low = (sector - 1 + 2 * core) * SECS
    count = listed(order, low, SECS, src, live[0, 0])
    add_listed(HALO_WIDTH, order, count, low, tgt, src, lbuf, rbuf, wave, acc, lambda j, state: state)

    q_rows = jnp.where(core == 0, 64, 16)
    c_rows = jnp.where(core == 0, 16, 64)
    row = lax.broadcasted_iota(jnp.int32, (16, BLOCK), 0)
    col = lax.broadcasted_iota(jnp.int32, (16, BLOCK), 1)

    def put(s, carry):
        size = sizes[s]
        for step, out in ((1, out_plus), (3, out_minus), (2, out_cross), (0, out_own)):
            to = c ^ step
            for q in range(4):
                at = pl.multiple_of(q * q_rows + to * c_rows, 16)
                piece = acc[s, pl.ds(at, 16), :]
                kept = jnp.maximum(row + at, col) < size
                out[s, q] = jnp.where(kept, piece, 0.0).astype(jnp.bfloat16)
        return carry

    lax.fori_loop(0, SECS, put, 0)


def merge_kernel(own, plus, minus, cross, mine, to_plus, to_minus, to_cross):
    _, core, y, x = place()
    c = jnp.where(core == 0, y, x)

    def put(s, carry):
        for step, out in ((1, to_plus), (3, to_minus), (2, to_cross), (0, mine)):
            at = c ^ step
            pieces = [ref[s, at].astype(jnp.float32) for ref in (own, plus, minus, cross)]
            out[s] = (pieces[0] + pieces[1] + (pieces[2] + pieces[3])).astype(out.dtype)
        return carry

    lax.fori_loop(0, SECS, put, 0)


def merge(*pieces):
    message = jax.ShapeDtypeStruct((SECS, 16, BLOCK), jnp.bfloat16)
    return pl.pallas_call(
        merge_kernel,
        in_specs=[VMEM] * 4,
        out_specs=[VMEM] * 4,
        out_shape=[jax.ShapeDtypeStruct((SECS, 16, BLOCK), jnp.float32)] + [message] * 3,
        compiler_params=PARAMS,
        name="merge",
    )(*pieces)


def last_kernel(mine, plus, minus, cross, out):
    pieces = [ref[...].astype(jnp.float32) for ref in (mine, plus, minus, cross)]
    out[...] = pieces[0] + pieces[1] + (pieces[2] + pieces[3])


def last_sum(*pieces):
    return pl.pallas_call(
        last_kernel,
        in_specs=[VMEM] * 4,
        out_specs=VMEM,
        out_shape=jax.ShapeDtypeStruct((SECS, 16, BLOCK), jnp.float32),
        compiler_params=PARAMS,
        name="last_sum",
    )(*pieces)


ACC = jax.ShapeDtypeStruct((SECS + 1, BLOCK, BLOCK), jnp.float32)
COST = pl.CostEstimate(flops=2 * 16 * 2 * BLOCK**3, bytes_accessed=16 * 4 * BLOCK * BLOCK, transcendentals=0)
PARAMS = pltpu.CompilerParams(vmem_limit_bytes=VLIM)


def work_slots(tgt, src, live, left, right, masked, partner):
    return pl.pallas_call(
        work_kernel,
        in_specs=[SMEM] * 3 + [HBM] * 2 + [VMEM] * 2,
        out_specs=[VMEM] * 3,
        out_shape=[ACC, blocks(SLOTS), blocks(SLOTS)],
        scratch_shapes=[
            pltpu.VMEM((2 * SECS, BLOCK, BLOCK), jnp.bfloat16),
            pltpu.SMEM((SLOTS + 16,), jnp.int32),
            pltpu.SemaphoreType.DMA((SLOTS // CHUNK,)),
            pltpu.SemaphoreType.DMA((SLOTS // CHUNK,)),
        ],
        compiler_params=PARAMS,
        cost_estimate=COST,
        name="work_slots",
    )(tgt, src, live, left, right, masked, partner)


def halo_slots(tgt, src, live, sizes, left, right, own, plus, minus, far, before):
    message = jax.ShapeDtypeStruct((SECS, 4, 16, BLOCK), jnp.bfloat16)
    return pl.pallas_call(
        halo_kernel,
        in_specs=[SMEM] * 4 + [VMEM] * 7,
        out_specs=[VMEM] * 5,
        out_shape=[ACC] + [message] * 4,
        scratch_shapes=[
            pltpu.VMEM((SECS, BLOCK, BLOCK), jnp.bfloat16),
            pltpu.SMEM((SLOTS + 16,), jnp.int32),
        ],
        input_output_aliases={10: 0},
        compiler_params=PARAMS,
        cost_estimate=COST,
        name="halo_slots",
    )(tgt, src, live, sizes, left, right, own, plus, minus, far, before)


def on_device(psi, sector_sizes, left_env, right_env, target, source, live_count):
    target = target.reshape(SLOTS)
    source = source.reshape(SLOTS)
    live = jnp.pad(live_count, ((0, 7), (0, 127)))
    left_env, right_env, psi, sizes = [
        pltpu.with_memory_space_constraint(v, pltpu.HBM)
        for v in (left_env, right_env, psi, sector_sizes)
    ]
    near, masked, far = near_blocks(psi, sizes)
    h_near = send(near, between_chips_pairs())
    masked, far = prep(psi, sizes, masked, far)
    h_far = send(far, between_chips_pairs())
    from_partner = send(masked, partner_pairs())
    h_plus = send(h_near, line_pairs(1, True))
    h_minus = send(h_near, line_pairs(3, True))
    total, left, right = work_slots(target, source, live, left_env, right_env, masked, from_partner)
    _, m_own, m_plus, m_minus, m_cross = halo_slots(
        target, source, live, sector_sizes, left, right,
        h_near, h_plus, h_minus, h_far, total,
    )
    g_cross = send(m_cross, line_pairs(2, True))
    g_plus = send(m_plus, line_pairs(1, True))
    g_minus = send(m_minus, line_pairs(3, True))
    mine, s_plus, s_minus, s_cross = merge(m_own, g_plus, g_minus, g_cross)
    t_cross = send(s_cross, line_pairs(2, False))
    t_plus = send(s_plus, line_pairs(1, False))
    t_minus = send(s_minus, line_pairs(3, False))
    return last_sum(mine, t_plus, t_minus, t_cross)


def solution(mesh):
    placed = (
        P("sector", None, None),
        P("sector"),
        P("term", "sector", None, None),
        P("term", "sector", None, None),
        P("term", "sector"),
        P("term", "sector"),
        P("term", "sector"),
    )
    return jax.shard_map(
        on_device, mesh=mesh, in_specs=placed, out_specs=P("sector", "term", None), check_vma=False
    )
```

time: 66.4 us -> 65.5 us (0.986)
  the two profiles are of different devices: /device:TPU:224 before, /device:TPU:128 now
where the time goes in v2:
time: 65.5 us; the launch traced here: 65.3 us
  waiting for transfers between devices  33 us (50%)
  starting transfers between devices  18.4 us (28%)
  Pallas kernels  13.2 us (20%)
  between operations  0.77 us (1%)
    ppermute x11, waiting for transfers between devices, send(): return lax.ppermute(x, AXES, pairs)  33 us
    ppermute x11, starting transfers between devices, send(): return lax.ppermute(x, AXES, pairs)  18.4 us
    pallas_call x1, Pallas kernels, work_slots(): pl.pallas_call(work_kernel, in_specs=[SMEM] * 3 + [HBM] * 2 + [VMEM] * 2,...  6.17 us
    pallas_call x1, Pallas kernels, halo_slots(): pl.pallas_call(halo_kernel, in_specs=[SMEM] * 4 + [VMEM] * 7, out_specs=[...  2.81 us
    pallas_call x1, Pallas kernels, prep(): pl.pallas_call(prep_kernel, in_specs=[HBM] * 2 + [VMEM] * 2, out_specs=[V...  1.86 us
  transfers between devices with their start and end apart: 11, of which 7 were waited for; matrix products, arithmetic and copies ran while one was open for 0% of the time, Pallas kernels for 9%

profile of v2, /device:TPU:128, one launch (start us, length us, event | category | flops | bytes accessed | tf_op | source)
XLA Modules:
  0.0 65.3 jit_solution(226447634472140385)
XLA Ops:
  0.0 0.0 copy-start.2
  0.0 0.0 copy-start.1
  0.0 1.2 %near_blocks.1 = (bf16[3,256,256]{2,1,0:T(8,128)(2,1)S(1)}, bf16[16,256,256]{2,1,0:T(8,128)(2,1)S(1)}, bf16[7,256,256]{2,1,0:T(8,128)(2,1)S(1)}) custom-call(s32[16]{0:T(128)} %sizes.1, bf16[16,256,256]{2,1,0:T(8,128)(2,1)} %psi.3), custom_call_target="tpu_custom_call" | custom-call | tf_op jit(solution)/shard_map/near_blocks/pallas_call | solution.py:147
  1.3 1.9 %prep.1 = (bf16[16,256,256]{2,1,0:T(8,128)(2,1)S(1)}, bf16[7,256,256]{2,1,0:T(8,128)(2,1)S(1)}) custom-call(s32[16]{0:T(128)} %sizes.1, bf16[16,256,256]{2,1,0:T(8,128)(2,1)} %psi.3, bf16[16,256,256]{2,1,0:T(8,128)(2,1)S(1)} %get-tuple-element.21.masked_in, ...), custom_call_target="tpu_custom_call", output_to_operand_aliasing={{0}: (2, {}), {1}: (3, {})} | custom-call | tf_op jit(solution)/shard_map/prep/pallas_call | solution.py:159
  3.1 0.1 collective-permute-start
  3.2 2.1 %collective-permute-start.4 = (bf16[7,256,256]{2,1,0:T(8,128)(2,1)S(1)}, bf16[7,256,256]{2,1,0:T(8,128)(2,1)S(1)}, u32[]{:S(2)}, u32[]{:S(2)}) collective-permute-start(bf16[7,256,256]{2,1,0:T(8,128)(2,1)S(1)} %get-tuple-element.27), channel_id=1, source_target_pairs={{16,32},{17,33},{18,34},{19,35},{20,36},{21,37},{22,38},{23,39},{2... | collective-permute-start | bytes 2752520 | tf_op jit(solution)/shard_map/ppermute | solution.py:57
  5.3 4.7 %collective-permute-start.1 = (bf16[3,256,256]{2,1,0:T(8,128)(2,1)S(1)}, bf16[3,256,256]{2,1,0:T(8,128)(2,1)S(1)}, u32[]{:S(2)}, u32[]{:S(2)}) collective-permute-start(bf16[3,256,256]{2,1,0:T(8,128)(2,1)S(1)} %get-tuple-element.26), channel_id=1, source_target_pairs={{16,32},{17,33},{18,34},{19,35},{20,36},{21,37},{22,38},{23,39},{2... | collective-permute-start | bytes 1179656 | tf_op jit(solution)/shard_map/ppermute | solution.py:57
  10.0 13.3 %collective-permute-done.1.own = bf16[3,256,256]{2,1,0:T(8,128)(2,1)S(1)} collective-permute-done((bf16[3,256,256]{2,1,0:T(8,128)(2,1)S(1)}, bf16[3,256,256]{2,1,0:T(8,128)(2,1)S(1)}, u32[]{:S(2)}, u32[]{:S(2)}) %collective-permute-start.1) | collective-permute-done | bytes 393248 | tf_op jit(solution)/shard_map/ppermute | solution.py:57
  23.4 2.8 %collective-permute-start.3 = (bf16[3,256,256]{2,1,0:T(8,128)(2,1)S(1)}, bf16[3,256,256]{2,1,0:T(8,128)(2,1)S(1)}, u32[]{:S(2)}, u32[]{:S(2)}) collective-permute-start(bf16[3,256,256]{2,1,0:T(8,128)(2,1)S(1)} %collective-permute-done.1.own), channel_id=1, source_target_pairs={{0,3},{1,2},{2,1},{3,0},{4,7},{5,6},{6,5},{7,4},{8,11},{9,10},{10,... | collective-permute-start | bytes 1179656 | tf_op jit(solution)/shard_map/ppermute | solution.py:57
  26.1 0.2 collective-permute-start.2
  27.0 0.0 collective-permute-done.partner
  27.0 0.0 copy-done.2
  27.0 0.0 copy-done.1
  27.0 0.0 copy-start
  27.0 6.2 %work_slots.1 = (f32[17,256,256]{2,1,0:T(8,128)S(1)}, bf16[48,256,256]{2,1,0:T(8,128)(2,1)S(1)}, bf16[48,256,256]{2,1,0:T(8,128)(2,1)S(1)}) custom-call(s32[48]{0:T(128)S(1)} %bitcast.2, s32[48]{0:T(128)S(1)} %bitcast.4, s32[8,128]{1,0:T(8,128)S(1)} %pad.4.live, bf16[48,1,256,256]{3,2,1,0:T(8,128)(2,1)} %left.1, bf16[48,1,256,256]{3,2,1,0:T(8,128)(2,1)} %right.1, ...), custom_call_target="tpu_custom_call" | custom-call | flops 1073741824 | bytes 4194304 | tf_op jit(solution)/shard_map/work_slots/pallas_call | solution.py:322
  33.2 0.0 collective-permute-done.3.minus
  33.2 0.7 %collective-permute-done.2.plus = bf16[3,256,256]{2,1,0:T(8,128)(2,1)S(1)} collective-permute-done((bf16[3,256,256]{2,1,0:T(8,128)(2,1)S(1)}, bf16[3,256,256]{2,1,0:T(8,128)(2,1)S(1)}, u32[]{:S(2)}, u32[]{:S(2)}) %collective-permute-start.2) | collective-permute-done | bytes 393248 | tf_op jit(solution)/shard_map/ppermute | solution.py:57
  33.9 0.0 collective-permute-done.4.far
  33.9 0.0 copy-done
  33.9 2.8 %halo_slots.1 = (f32[17,256,256]{2,1,0:T(8,128)S(1)}, bf16[16,4,16,256]{3,2,1,0:T(8,128)(2,1)S(1)}, bf16[16,4,16,256]{3,2,1,0:T(8,128)(2,1)S(1)}, bf16[16,4,16,2...) custom-call(s32[48]{0:T(128)S(1)} %bitcast.3, s32[48]{0:T(128)S(1)} %bitcast.5, ...), custom_call_target="tpu_custom_call", output_to_operand_aliasing={{0}: (10, {})} | custom-call | flops 1073741824 | bytes 4194304 | tf_op jit(solution)/shard_map/halo_slots/pallas_call | solution.py:341
  36.7 0.7 %collective-permute-start.5 = (bf16[16,4,16,256]{3,2,1,0:T(8,128)(2,1)S(1)}, bf16[16,4,16,256]{3,2,1,0:T(8,128)(2,1)S(1)}, u32[]{:S(2)}, u32[]{:S(2)}) collective-permute-start(bf16[16,4,16,256]{3,2,1,0:T(8,128)(2,1)S(1)} %get-tuple-element.30), channel_id=1, source_target_pairs={{0,1},{1,0},{2,3},{3,2},{4,5},{5,4},{6,7},{7,6},{8,9},{9,8},{10,11... | collective-permute-start | bytes 1572872 | tf_op jit(solution)/shard_map/ppermute | solution.py:57
  37.4 0.7 %collective-permute-start.6 = (bf16[16,4,16,256]{3,2,1,0:T(8,128)(2,1)S(1)}, bf16[16,4,16,256]{3,2,1,0:T(8,128)(2,1)S(1)}, u32[]{:S(2)}, u32[]{:S(2)}) collective-permute-start(bf16[16,4,16,256]{3,2,1,0:T(8,128)(2,1)S(1)} %get-tuple-element.31), channel_id=1, source_target_pairs={{0,3},{1,2},{2,1},{3,0},{4,7},{5,6},{6,5},{7,4},{8,11},{9,10},{10,... | collective-permute-start | bytes 1572872 | tf_op jit(solution)/shard_map/ppermute | solution.py:57
  38.1 2.8 %collective-permute-start.7 = (bf16[16,4,16,256]{3,2,1,0:T(8,128)(2,1)S(1)}, bf16[16,4,16,256]{3,2,1,0:T(8,128)(2,1)S(1)}, u32[]{:S(2)}, u32[]{:S(2)}) collective-permute-start(bf16[16,4,16,256]{3,2,1,0:T(8,128)(2,1)S(1)} %get-tuple-element.32), channel_id=1, source_target_pairs={{0,2},{1,3},{2,0},{3,1},{4,6},{5,7},{6,4},{7,5},{8,10},{9,11},{10,... | collective-permute-start | bytes 1572872 | tf_op jit(solution)/shard_map/ppermute | solution.py:57
  40.9 5.1 %collective-permute-done.5.plus = bf16[16,4,16,256]{3,2,1,0:T(8,128)(2,1)S(1)} collective-permute-done((bf16[16,4,16,256]{3,2,1,0:T(8,128)(2,1)S(1)}, bf16[16,4,16,256]{3,2,1,0:T(8,128)(2,1)S(1)}, u32[]{:S(2)}, u32[]{:S(2)}) %collective-permute-start.5) | collective-permute-done | bytes 524320 | tf_op jit(solution)/shard_map/ppermute | solution.py:57
  46.0 7.4 %collective-permute-done.6.minus = bf16[16,4,16,256]{3,2,1,0:T(8,128)(2,1)S(1)} collective-permute-done((bf16[16,4,16,256]{3,2,1,0:T(8,128)(2,1)S(1)}, bf16[16,4,16,256]{3,2,1,0:T(8,128)(2,1)S(1)}, u32[]{:S(2)}, u32[]{:S(2)}) %collective-permute-start.6) | collective-permute-done | bytes 524320 | tf_op jit(solution)/shard_map/ppermute | solution.py:57
  53.4 0.0 collective-permute-done.7.cross
  53.4 0.3 merge.1
  53.8 1.7 %collective-permute-start.8 = (bf16[16,16,256]{2,1,0:T(8,128)(2,1)S(1)}, bf16[16,16,256]{2,1,0:T(8,128)(2,1)S(1)}, u32[]{:S(2)}, u32[]{:S(2)}) collective-permute-start(bf16[16,16,256]{2,1,0:T(8,128)(2,1)S(1)} %get-tuple-element.34), channel_id=1, source_target_pairs={{0,4},{1,5},{2,6},{3,7},{4,0},{5,1},{6,2},{7,3},{8,12},{9,13},{10,... | collective-permute-start | bytes 393224 | tf_op jit(solution)/shard_map/ppermute | solution.py:57
  55.5 2.6 %collective-permute-start.9 = (bf16[16,16,256]{2,1,0:T(8,128)(2,1)S(1)}, bf16[16,16,256]{2,1,0:T(8,128)(2,1)S(1)}, u32[]{:S(2)}, u32[]{:S(2)}) collective-permute-start(bf16[16,16,256]{2,1,0:T(8,128)(2,1)S(1)} %get-tuple-element.35), channel_id=1, source_target_pairs={{0,12},{1,13},{2,14},{3,15},{4,8},{5,9},{6,10},{7,11},{8,4},{9,5},... | collective-permute-start | bytes 393224 | tf_op jit(solution)/shard_map/ppermute | solution.py:57
  58.1 0.0 collective-permute-start.10
  58.1 0.7 %collective-permute-done.8.plus = bf16[16,16,256]{2,1,0:T(8,128)(2,1)S(1)} collective-permute-done((bf16[16,16,256]{2,1,0:T(8,128)(2,1)S(1)}, bf16[16,16,256]{2,1,0:T(8,128)(2,1)S(1)}, u32[]{:S(2)}, u32[]{:S(2)}) %collective-permute-start.8) | collective-permute-done | bytes 131104 | tf_op jit(solution)/shard_map/ppermute | solution.py:57
  58.8 3.2 %collective-permute-done.9.minus = bf16[16,16,256]{2,1,0:T(8,128)(2,1)S(1)} collective-permute-done((bf16[16,16,256]{2,1,0:T(8,128)(2,1)S(1)}, bf16[16,16,256]{2,1,0:T(8,128)(2,1)S(1)}, u32[]{:S(2)}, u32[]{:S(2)}) %collective-permute-start.9) | collective-permute-done | bytes 131104 | tf_op jit(solution)/shard_map/ppermute | solution.py:57
  62.0 2.5 %collective-permute-done.10.cross = bf16[16,16,256]{2,1,0:T(8,128)(2,1)S(1)} collective-permute-done((bf16[16,16,256]{2,1,0:T(8,128)(2,1)S(1)}, bf16[16,16,256]{2,1,0:T(8,128)(2,1)S(1)}, u32[]{:S(2)}, u32[]{:S(2)}) %collective-permute-start.10) | collective-permute-done | bytes 131104 | tf_op jit(solution)/shard_map/ppermute | solution.py:57
  64.6 0.8 %last_sum.1 = f32[16,16,256]{2,1,0:T(8,128)} custom-call(f32[16,16,256]{2,1,0:T(8,128)S(1)} %get-tuple-element.33.mine, bf16[16,16,256]{2,1,0:T(8,128)(2,1)S(1)} %collective-permute-done.8.plus, bf16[16,16,256]{2,1,0:T(8,128)(2,1)S(1)} %collective-permute-done.9.minus, bf16[16,16,256]{2,1,0:T(8,128)(2,1)S(1)} %collective-permute-done.10.cross), custom_call_target="tpu_custom_call" | custom-call | tf_op jit(solution)/shard_map/last_sum/pallas_call | solution.py:306
  (1 shorter events, 0.0 us)
Async XLA Ops:
  0.0 27.0 %copy-start.2 = (s32[48,1]{0,1:T(1,128)S(1)}, s32[48,1]{0,1:T(1,128)}, u32[]{:S(2)}) copy-start(s32[48,1]{0,1:T(1,128)} %param.12) | copy-start | bytes 580
  0.0 27.0 %copy-start.1 = (s32[48,1]{0,1:T(1,128)S(1)}, s32[48,1]{0,1:T(1,128)}, u32[]{:S(2)}) copy-start(s32[48,1]{0,1:T(1,128)} %param.11) | copy-start | bytes 580
  3.1 23.9 %collective-permute-start = (bf16[16,256,256]{2,1,0:T(8,128)(2,1)S(1)}, bf16[16,256,256]{2,1,0:T(8,128)(2,1)S(1)}, u32[]{:S(2)}, u32[]{:S(2)}) collective-permute-start(bf16[16,256,256]{2,1,0:T(8,128)(2,1)S(1)} %get-tuple-element.23.masked), channel_id=1, source_target_pairs={{0,16},{1,17},{2,18},{3,19},{4,20},{5,21},{6,22},{7,23},{8,24},{9,... | collective-permute-start | bytes 6291464 | tf_op jit(solution)/shard_map/ppermute | solution.py:57
  3.2 30.7 %collective-permute-start.4 = (bf16[7,256,256]{2,1,0:T(8,128)(2,1)S(1)}, bf16[7,256,256]{2,1,0:T(8,128)(2,1)S(1)}, u32[]{:S(2)}, u32[]{:S(2)}) collective-permute-start(bf16[7,256,256]{2,1,0:T(8,128)(2,1)S(1)} %get-tuple-element.27), channel_id=1, source_target_pairs={{16,32},{17,33},{18,34},{19,35},{20,36},{21,37},{22,38},{23,39},{2... | collective-permute-start | bytes 2752520 | tf_op jit(solution)/shard_map/ppermute | solution.py:57
  5.3 18.0 %collective-permute-start.1 = (bf16[3,256,256]{2,1,0:T(8,128)(2,1)S(1)}, bf16[3,256,256]{2,1,0:T(8,128)(2,1)S(1)}, u32[]{:S(2)}, u32[]{:S(2)}) collective-permute-start(bf16[3,256,256]{2,1,0:T(8,128)(2,1)S(1)} %get-tuple-element.26), channel_id=1, source_target_pairs={{16,32},{17,33},{18,34},{19,35},{20,36},{21,37},{22,38},{23,39},{2... | collective-permute-start | bytes 1179656 | tf_op jit(solution)/shard_map/ppermute | solution.py:57
  23.4 9.9 %collective-permute-start.3 = (bf16[3,256,256]{2,1,0:T(8,128)(2,1)S(1)}, bf16[3,256,256]{2,1,0:T(8,128)(2,1)S(1)}, u32[]{:S(2)}, u32[]{:S(2)}) collective-permute-start(bf16[3,256,256]{2,1,0:T(8,128)(2,1)S(1)} %collective-permute-done.1.own), channel_id=1, source_target_pairs={{0,3},{1,2},{2,1},{3,0},{4,7},{5,6},{6,5},{7,4},{8,11},{9,10},{10,... | collective-permute-start | bytes 1179656 | tf_op jit(solution)/shard_map/ppermute | solution.py:57
  26.1 7.8 %collective-permute-start.2 = (bf16[3,256,256]{2,1,0:T(8,128)(2,1)S(1)}, bf16[3,256,256]{2,1,0:T(8,128)(2,1)S(1)}, u32[]{:S(2)}, u32[]{:S(2)}) collective-permute-start(bf16[3,256,256]{2,1,0:T(8,128)(2,1)S(1)} %collective-permute-done.1.own), channel_id=1, source_target_pairs={{0,1},{1,0},{2,3},{3,2},{4,5},{5,4},{6,7},{7,6},{8,9},{9,8},{10,11... | collective-permute-start | bytes 1179656 | tf_op jit(solution)/shard_map/ppermute | solution.py:57
  27.0 6.9 %copy-start = (s32[16]{0:T(128)S(1)}, s32[16]{0:T(128)}, u32[]{:S(2)}) copy-start(s32[16]{0:T(128)} %sizes.1) | copy-start | bytes 196
  36.7 9.3 %collective-permute-start.5 = (bf16[16,4,16,256]{3,2,1,0:T(8,128)(2,1)S(1)}, bf16[16,4,16,256]{3,2,1,0:T(8,128)(2,1)S(1)}, u32[]{:S(2)}, u32[]{:S(2)}) collective-permute-start(bf16[16,4,16,256]{3,2,1,0:T(8,128)(2,1)S(1)} %get-tuple-element.30), channel_id=1, source_target_pairs={{0,1},{1,0},{2,3},{3,2},{4,5},{5,4},{6,7},{7,6},{8,9},{9,8},{10,11... | collective-permute-start | bytes 1572872 | tf_op jit(solution)/shard_map/ppermute | solution.py:57
  37.4 16.0 %collective-permute-start.6 = (bf16[16,4,16,256]{3,2,1,0:T(8,128)(2,1)S(1)}, bf16[16,4,16,256]{3,2,1,0:T(8,128)(2,1)S(1)}, u32[]{:S(2)}, u32[]{:S(2)}) collective-permute-start(bf16[16,4,16,256]{3,2,1,0:T(8,128)(2,1)S(1)} %get-tuple-element.31), channel_id=1, source_target_pairs={{0,3},{1,2},{2,1},{3,0},{4,7},{5,6},{6,5},{7,4},{8,11},{9,10},{10,... | collective-permute-start | bytes 1572872 | tf_op jit(solution)/shard_map/ppermute | solution.py:57
  38.1 15.3 %collective-permute-start.7 = (bf16[16,4,16,256]{3,2,1,0:T(8,128)(2,1)S(1)}, bf16[16,4,16,256]{3,2,1,0:T(8,128)(2,1)S(1)}, u32[]{:S(2)}, u32[]{:S(2)}) collective-permute-start(bf16[16,4,16,256]{3,2,1,0:T(8,128)(2,1)S(1)} %get-tuple-element.32), channel_id=1, source_target_pairs={{0,2},{1,3},{2,0},{3,1},{4,6},{5,7},{6,4},{7,5},{8,10},{9,11},{10,... | collective-permute-start | bytes 1572872 | tf_op jit(solution)/shard_map/ppermute | solution.py:57
  53.8 5.1 %collective-permute-start.8 = (bf16[16,16,256]{2,1,0:T(8,128)(2,1)S(1)}, bf16[16,16,256]{2,1,0:T(8,128)(2,1)S(1)}, u32[]{:S(2)}, u32[]{:S(2)}) collective-permute-start(bf16[16,16,256]{2,1,0:T(8,128)(2,1)S(1)} %get-tuple-element.34), channel_id=1, source_target_pairs={{0,4},{1,5},{2,6},{3,7},{4,0},{5,1},{6,2},{7,3},{8,12},{9,13},{10,... | collective-permute-start | bytes 393224 | tf_op jit(solution)/shard_map/ppermute | solution.py:57
  55.5 6.6 %collective-permute-start.9 = (bf16[16,16,256]{2,1,0:T(8,128)(2,1)S(1)}, bf16[16,16,256]{2,1,0:T(8,128)(2,1)S(1)}, u32[]{:S(2)}, u32[]{:S(2)}) collective-permute-start(bf16[16,16,256]{2,1,0:T(8,128)(2,1)S(1)} %get-tuple-element.35), channel_id=1, source_target_pairs={{0,12},{1,13},{2,14},{3,15},{4,8},{5,9},{6,10},{7,11},{8,4},{9,5},... | collective-permute-start | bytes 393224 | tf_op jit(solution)/shard_map/ppermute | solution.py:57
  58.1 6.5 %collective-permute-start.10 = (bf16[16,16,256]{2,1,0:T(8,128)(2,1)S(1)}, bf16[16,16,256]{2,1,0:T(8,128)(2,1)S(1)}, u32[]{:S(2)}, u32[]{:S(2)}) collective-permute-start(bf16[16,16,256]{2,1,0:T(8,128)(2,1)S(1)} %get-tuple-element.36), channel_id=1, source_target_pairs={{0,8},{1,9},{2,10},{3,11},{4,12},{5,13},{6,14},{7,15},{8,0},{9,1},... | collective-permute-start | bytes 393224 | tf_op jit(solution)/shard_map/ppermute | solution.py:57

commit v3 on v2

--- a/solution.py
+++ b/solution.py
@@ -199,7 +199,10 @@
     return lax.fori_loop(0, (count + width - 1) // width, step, jnp.int32(0))
 
 
-def work_kernel(tgt, src, live, left, right, masked, partner, acc, lbuf, rbuf, wave, order, lsem, rsem):
+def work_kernel(
+    tgt, src, live, sizes, left, right, masked, partner,
+    acc, lbuf, rbuf, keep, wave, order, lsem, rsem,
+):
     def fetches(k):
         at = pl.ds(k * CHUNK, CHUNK)
         return (
@@ -212,11 +215,15 @@
             copy.start()
     sector, core, _, _ = place()
     low = (sector - core) * SECS
+    row = lax.broadcasted_iota(jnp.int32, (16, BLOCK), 0) + 16 * lax.axis_index("term")
+    col = lax.broadcasted_iota(jnp.int32, (16, BLOCK), 1)
+    most = jnp.maximum(row, col)
 
     def fill(s, carry):
         acc[s] = jnp.zeros((BLOCK, BLOCK), jnp.float32)
         wave[core * SECS + s] = masked[s]
         wave[(1 - core) * SECS + s] = partner[s]
+        keep[s] = (most < sizes[s]).astype(jnp.float32)
         return carry
 
     lax.fori_loop(0, SECS, fill, 0)
@@ -237,7 +244,7 @@
 
 
 def halo_kernel(
-    tgt, src, live, sizes, lbuf, rbuf, own, plus, minus, far, before,
+    tgt, src, live, lbuf, rbuf, own, plus, minus, far, before,
     acc, out_own, out_plus, out_minus, out_cross,
     wave, order,
 ):
@@ -254,18 +261,13 @@
 
     q_rows = jnp.where(core == 0, 64, 16)
     c_rows = jnp.where(core == 0, 16, 64)
-    row = lax.broadcasted_iota(jnp.int32, (16, BLOCK), 0)
-    col = lax.broadcasted_iota(jnp.int32, (16, BLOCK), 1)
 
     def put(s, carry):
-        size = sizes[s]
         for step, out in ((1, out_plus), (3, out_minus), (2, out_cross), (0, out_own)):
             to = c ^ step
             for q in range(4):
                 at = pl.multiple_of(q * q_rows + to * c_rows, 16)
-                piece = acc[s, pl.ds(at, 16), :]
-                kept = jnp.maximum(row + at, col) < size
-                out[s, q] = jnp.where(kept, piece, 0.0).astype(jnp.bfloat16)
+                out[s, q] = acc[s, pl.ds(at, 16), :].astype(jnp.bfloat16)
         return carry
 
     lax.fori_loop(0, SECS, put, 0)
@@ -297,15 +299,16 @@
     )(*pieces)
 
 
-def last_kernel(mine, plus, minus, cross, out):
+def last_kernel(keep, mine, plus, minus, cross, out):
     pieces = [ref[...].astype(jnp.float32) for ref in (mine, plus, minus, cross)]
-    out[...] = pieces[0] + pieces[1] + (pieces[2] + pieces[3])
+    total = pieces[0] + pieces[1] + (pieces[2] + pieces[3])
+    out[...] = jnp.where(keep[...] > 0.0, total, 0.0)
 
 
 def last_sum(*pieces):
     return pl.pallas_call(
         last_kernel,
-        in_specs=[VMEM] * 4,
+        in_specs=[VMEM] * 5,
         out_specs=VMEM,
         out_shape=jax.ShapeDtypeStruct((SECS, 16, BLOCK), jnp.float32),
         compiler_params=PARAMS,
@@ -313,17 +316,18 @@
     )(*pieces)
 
 
+ROWS = jax.ShapeDtypeStruct((SECS, 16, BLOCK), jnp.float32)
 ACC = jax.ShapeDtypeStruct((SECS + 1, BLOCK, BLOCK), jnp.float32)
 COST = pl.CostEstimate(flops=2 * 16 * 2 * BLOCK**3, bytes_accessed=16 * 4 * BLOCK * BLOCK, transcendentals=0)
 PARAMS = pltpu.CompilerParams(vmem_limit_bytes=VLIM)
 
 
-def work_slots(tgt, src, live, left, right, masked, partner):
+def work_slots(tgt, src, live, sizes, left, right, masked, partner):
     return pl.pallas_call(
         work_kernel,
-        in_specs=[SMEM] * 3 + [HBM] * 2 + [VMEM] * 2,
-        out_specs=[VMEM] * 3,
-        out_shape=[ACC, blocks(SLOTS), blocks(SLOTS)],
+        in_specs=[SMEM] * 4 + [HBM] * 2 + [VMEM] * 2,
+        out_specs=[VMEM] * 4,
+        out_shape=[ACC, blocks(SLOTS), blocks(SLOTS), ROWS],
         scratch_shapes=[
             pltpu.VMEM((2 * SECS, BLOCK, BLOCK), jnp.bfloat16),
             pltpu.SMEM((SLOTS + 16,), jnp.int32),
@@ -333,25 +337,25 @@
         compiler_params=PARAMS,
         cost_estimate=COST,
         name="work_slots",
-    )(tgt, src, live, left, right, masked, partner)
-
-
-def halo_slots(tgt, src, live, sizes, left, right, own, plus, minus, far, before):
+    )(tgt, src, live, sizes, left, right, masked, partner)
+
+
+def halo_slots(tgt, src, live, left, right, own, plus, minus, far, before):
     message = jax.ShapeDtypeStruct((SECS, 4, 16, BLOCK), jnp.bfloat16)
     return pl.pallas_call(
         halo_kernel,
-        in_specs=[SMEM] * 4 + [VMEM] * 7,
+        in_specs=[SMEM] * 3 + [VMEM] * 7,
         out_specs=[VMEM] * 5,
         out_shape=[ACC] + [message] * 4,
         scratch_shapes=[
             pltpu.VMEM((SECS, BLOCK, BLOCK), jnp.bfloat16),
             pltpu.SMEM((SLOTS + 16,), jnp.int32),
         ],
-        input_output_aliases={10: 0},
+        input_output_aliases={9: 0},
         compiler_params=PARAMS,
         cost_estimate=COST,
         name="halo_slots",
-    )(tgt, src, live, sizes, left, right, own, plus, minus, far, before)
+    )(tgt, src, live, left, right, own, plus, minus, far, before)
 
 
 def on_device(psi, sector_sizes, left_env, right_env, target, source, live_count):
@@ -369,9 +373,11 @@
     from_partner = send(masked, partner_pairs())
     h_plus = send(h_near, line_pairs(1, True))
     h_minus = send(h_near, line_pairs(3, True))
-    total, left, right = work_slots(target, source, live, left_env, right_env, masked, from_partner)
+    total, left, right, keep = work_slots(
+        target, source, live, sector_sizes, left_env, right_env, masked, from_partner
+    )
     _, m_own, m_plus, m_minus, m_cross = halo_slots(
-        target, source, live, sector_sizes, left, right,
+        target, source, live, left, right,
         h_near, h_plus, h_minus, h_far, total,
     )
     g_cross = send(m_cross, line_pairs(2, True))
@@ -381,7 +387,7 @@
     t_cross = send(s_cross, line_pairs(2, False))
     t_plus = send(s_plus, line_pairs(1, False))
     t_minus = send(s_minus, line_pairs(3, False))
-    return last_sum(mine, t_plus, t_minus, t_cross)
+    return last_sum(keep, mine, t_plus, t_minus, t_cross)
 
 
 def solution(mesh):

time: 65.5 us -> 65.2 us (level)
  no operation moved by 1% of the time
where the time goes in v3:
time: 65.2 us; the launch traced here: 65 us
  waiting for transfers between devices  33 us (51%)
  starting transfers between devices  18.4 us (28%)
  Pallas kernels  12.9 us (20%)
  between operations  0.78 us (1%)
    ppermute x11, waiting for transfers between devices, send(): return lax.ppermute(x, AXES, pairs)  33 us
    ppermute x11, starting transfers between devices, send(): return lax.ppermute(x, AXES, pairs)  18.4 us
    pallas_call x1, Pallas kernels, work_slots(): pl.pallas_call(work_kernel, in_specs=[SMEM] * 4 + [HBM] * 2 + [VMEM] * 2,...  6.13 us
    pallas_call x1, Pallas kernels, halo_slots(): pl.pallas_call(halo_kernel, in_specs=[SMEM] * 3 + [VMEM] * 7, out_specs=[...  2.5 us
    pallas_call x1, Pallas kernels, prep(): pl.pallas_call(prep_kernel, in_specs=[HBM] * 2 + [VMEM] * 2, out_specs=[V...  1.86 us
  transfers between devices with their start and end apart: 11, of which 7 were waited for; matrix products, arithmetic and copies ran while one was open for 0% of the time, Pallas kernels for 9%

profile of v3, /device:TPU:128, one launch (start us, length us, event | category | flops | bytes accessed | tf_op | source)
XLA Modules:
  0.0 65.0 jit_solution(11097170569872793997)
XLA Ops:
  0.0 0.0 copy-start
  0.0 0.0 copy-start.2
  0.0 0.0 copy-start.1
  0.0 1.3 %near_blocks.1 = (bf16[3,256,256]{2,1,0:T(8,128)(2,1)S(1)}, bf16[16,256,256]{2,1,0:T(8,128)(2,1)S(1)}, bf16[7,256,256]{2,1,0:T(8,128)(2,1)S(1)}) custom-call(s32[16]{0:T(128)} %sizes.1, bf16[16,256,256]{2,1,0:T(8,128)(2,1)} %psi.3), custom_call_target="tpu_custom_call" | custom-call | tf_op jit(solution)/shard_map/near_blocks/pallas_call | solution.py:147
  1.3 1.9 %prep.1 = (bf16[16,256,256]{2,1,0:T(8,128)(2,1)S(1)}, bf16[7,256,256]{2,1,0:T(8,128)(2,1)S(1)}) custom-call(s32[16]{0:T(128)} %sizes.1, bf16[16,256,256]{2,1,0:T(8,128)(2,1)} %psi.3, bf16[16,256,256]{2,1,0:T(8,128)(2,1)S(1)} %get-tuple-element.22.masked_in, ...), custom_call_target="tpu_custom_call", output_to_operand_aliasing={{0}: (2, {}), {1}: (3, {})} | custom-call | tf_op jit(solution)/shard_map/prep/pallas_call | solution.py:159
  3.1 0.1 collective-permute-start
  3.2 2.1 %collective-permute-start.4 = (bf16[7,256,256]{2,1,0:T(8,128)(2,1)S(1)}, bf16[7,256,256]{2,1,0:T(8,128)(2,1)S(1)}, u32[]{:S(2)}, u32[]{:S(2)}) collective-permute-start(bf16[7,256,256]{2,1,0:T(8,128)(2,1)S(1)} %get-tuple-element.29), channel_id=1, source_target_pairs={{16,32},{17,33},{18,34},{19,35},{20,36},{21,37},{22,38},{23,39},{2... | collective-permute-start | bytes 2752520 | tf_op jit(solution)/shard_map/ppermute | solution.py:57
  5.3 4.7 %collective-permute-start.1 = (bf16[3,256,256]{2,1,0:T(8,128)(2,1)S(1)}, bf16[3,256,256]{2,1,0:T(8,128)(2,1)S(1)}, u32[]{:S(2)}, u32[]{:S(2)}) collective-permute-start(bf16[3,256,256]{2,1,0:T(8,128)(2,1)S(1)} %get-tuple-element.28), channel_id=1, source_target_pairs={{16,32},{17,33},{18,34},{19,35},{20,36},{21,37},{22,38},{23,39},{2... | collective-permute-start | bytes 1179656 | tf_op jit(solution)/shard_map/ppermute | solution.py:57
  10.0 13.3 %collective-permute-done.1.own = bf16[3,256,256]{2,1,0:T(8,128)(2,1)S(1)} collective-permute-done((bf16[3,256,256]{2,1,0:T(8,128)(2,1)S(1)}, bf16[3,256,256]{2,1,0:T(8,128)(2,1)S(1)}, u32[]{:S(2)}, u32[]{:S(2)}) %collective-permute-start.1) | collective-permute-done | bytes 393248 | tf_op jit(solution)/shard_map/ppermute | solution.py:57
  23.4 2.8 %collective-permute-start.3 = (bf16[3,256,256]{2,1,0:T(8,128)(2,1)S(1)}, bf16[3,256,256]{2,1,0:T(8,128)(2,1)S(1)}, u32[]{:S(2)}, u32[]{:S(2)}) collective-permute-start(bf16[3,256,256]{2,1,0:T(8,128)(2,1)S(1)} %collective-permute-done.1.own), channel_id=1, source_target_pairs={{0,3},{1,2},{2,1},{3,0},{4,7},{5,6},{6,5},{7,4},{8,11},{9,10},{10,... | collective-permute-start | bytes 1179656 | tf_op jit(solution)/shard_map/ppermute | solution.py:57
  26.1 0.2 collective-permute-start.2
  27.0 0.0 collective-permute-done.partner
  27.0 0.0 copy-done
  27.0 0.0 copy-done.2
  27.0 0.0 copy-done.1
  27.1 6.1 %work_slots.1 = (f32[17,256,256]{2,1,0:T(8,128)S(1)}, bf16[48,256,256]{2,1,0:T(8,128)(2,1)S(1)}, bf16[48,256,256]{2,1,0:T(8,128)(2,1)S(1)}, f32[16,16,256]{2,1,0:T(8,128)S(1)}) custom-call(s32[48]{0:T(128)S(1)} %bitcast.2, s32[48]{0:T(128)S(1)} %bitcast.4, s32[8,128]{1,0:T(8,128)S(1)} %pad.4.live, s32[16]{0:T(128)S(1)} %copy-done, ...), custom_call_target="tpu_custom_call" | custom-call | flops 1073741824 | bytes 4194304 | tf_op jit(solution)/shard_map/work_slots/pallas_call | solution.py:326
  33.2 0.0 collective-permute-done.3.minus
  33.2 0.7 %collective-permute-done.2.plus = bf16[3,256,256]{2,1,0:T(8,128)(2,1)S(1)} collective-permute-done((bf16[3,256,256]{2,1,0:T(8,128)(2,1)S(1)}, bf16[3,256,256]{2,1,0:T(8,128)(2,1)S(1)}, u32[]{:S(2)}, u32[]{:S(2)}) %collective-permute-start.2) | collective-permute-done | bytes 393248 | tf_op jit(solution)/shard_map/ppermute | solution.py:57
  33.9 0.0 collective-permute-done.4.far
  33.9 2.5 %halo_slots.1 = (f32[17,256,256]{2,1,0:T(8,128)S(1)}, bf16[16,4,16,256]{3,2,1,0:T(8,128)(2,1)S(1)}, bf16[16,4,16,256]{3,2,1,0:T(8,128)(2,1)S(1)}, bf16[16,4,16,2...) custom-call(s32[48]{0:T(128)S(1)} %bitcast.3, s32[48]{0:T(128)S(1)} %bitcast.5, ...), custom_call_target="tpu_custom_call", output_to_operand_aliasing={{0}: (9, {})} | custom-call | flops 1073741824 | bytes 4194304 | tf_op jit(solution)/shard_map/halo_slots/pallas_call | solution.py:345
  36.4 0.7 %collective-permute-start.5 = (bf16[16,4,16,256]{3,2,1,0:T(8,128)(2,1)S(1)}, bf16[16,4,16,256]{3,2,1,0:T(8,128)(2,1)S(1)}, u32[]{:S(2)}, u32[]{:S(2)}) collective-permute-start(bf16[16,4,16,256]{3,2,1,0:T(8,128)(2,1)S(1)} %get-tuple-element.32), channel_id=1, source_target_pairs={{0,1},{1,0},{2,3},{3,2},{4,5},{5,4},{6,7},{7,6},{8,9},{9,8},{10,11... | collective-permute-start | bytes 1572872 | tf_op jit(solution)/shard_map/ppermute | solution.py:57
  37.1 0.7 %collective-permute-start.6 = (bf16[16,4,16,256]{3,2,1,0:T(8,128)(2,1)S(1)}, bf16[16,4,16,256]{3,2,1,0:T(8,128)(2,1)S(1)}, u32[]{:S(2)}, u32[]{:S(2)}) collective-permute-start(bf16[16,4,16,256]{3,2,1,0:T(8,128)(2,1)S(1)} %get-tuple-element.33), channel_id=1, source_target_pairs={{0,3},{1,2},{2,1},{3,0},{4,7},{5,6},{6,5},{7,4},{8,11},{9,10},{10,... | collective-permute-start | bytes 1572872 | tf_op jit(solution)/shard_map/ppermute | solution.py:57
  37.8 2.8 %collective-permute-start.7 = (bf16[16,4,16,256]{3,2,1,0:T(8,128)(2,1)S(1)}, bf16[16,4,16,256]{3,2,1,0:T(8,128)(2,1)S(1)}, u32[]{:S(2)}, u32[]{:S(2)}) collective-permute-start(bf16[16,4,16,256]{3,2,1,0:T(8,128)(2,1)S(1)} %get-tuple-element.34), channel_id=1, source_target_pairs={{0,2},{1,3},{2,0},{3,1},{4,6},{5,7},{6,4},{7,5},{8,10},{9,11},{10,... | collective-permute-start | bytes 1572872 | tf_op jit(solution)/shard_map/ppermute | solution.py:57
  40.6 5.1 %collective-permute-done.5.plus = bf16[16,4,16,256]{3,2,1,0:T(8,128)(2,1)S(1)} collective-permute-done((bf16[16,4,16,256]{3,2,1,0:T(8,128)(2,1)S(1)}, bf16[16,4,16,256]{3,2,1,0:T(8,128)(2,1)S(1)}, u32[]{:S(2)}, u32[]{:S(2)}) %collective-permute-start.5) | collective-permute-done | bytes 524320 | tf_op jit(solution)/shard_map/ppermute | solution.py:57
  45.7 7.4 %collective-permute-done.6.minus = bf16[16,4,16,256]{3,2,1,0:T(8,128)(2,1)S(1)} collective-permute-done((bf16[16,4,16,256]{3,2,1,0:T(8,128)(2,1)S(1)}, bf16[16,4,16,256]{3,2,1,0:T(8,128)(2,1)S(1)}, u32[]{:S(2)}, u32[]{:S(2)}) %collective-permute-start.6) | collective-permute-done | bytes 524320 | tf_op jit(solution)/shard_map/ppermute | solution.py:57
  53.1 0.0 collective-permute-done.7.cross
  53.1 0.3 merge.1
  53.5 1.7 %collective-permute-start.8 = (bf16[16,16,256]{2,1,0:T(8,128)(2,1)S(1)}, bf16[16,16,256]{2,1,0:T(8,128)(2,1)S(1)}, u32[]{:S(2)}, u32[]{:S(2)}) collective-permute-start(bf16[16,16,256]{2,1,0:T(8,128)(2,1)S(1)} %get-tuple-element.36), channel_id=1, source_target_pairs={{0,4},{1,5},{2,6},{3,7},{4,0},{5,1},{6,2},{7,3},{8,12},{9,13},{10,... | collective-permute-start | bytes 393224 | tf_op jit(solution)/shard_map/ppermute | solution.py:57
  55.1 2.6 %collective-permute-start.9 = (bf16[16,16,256]{2,1,0:T(8,128)(2,1)S(1)}, bf16[16,16,256]{2,1,0:T(8,128)(2,1)S(1)}, u32[]{:S(2)}, u32[]{:S(2)}) collective-permute-start(bf16[16,16,256]{2,1,0:T(8,128)(2,1)S(1)} %get-tuple-element.37), channel_id=1, source_target_pairs={{0,12},{1,13},{2,14},{3,15},{4,8},{5,9},{6,10},{7,11},{8,4},{9,5},... | collective-permute-start | bytes 393224 | tf_op jit(solution)/shard_map/ppermute | solution.py:57
  57.8 0.1 collective-permute-start.10
  57.8 0.7 %collective-permute-done.8.plus = bf16[16,16,256]{2,1,0:T(8,128)(2,1)S(1)} collective-permute-done((bf16[16,16,256]{2,1,0:T(8,128)(2,1)S(1)}, bf16[16,16,256]{2,1,0:T(8,128)(2,1)S(1)}, u32[]{:S(2)}, u32[]{:S(2)}) %collective-permute-start.8) | collective-permute-done | bytes 131104 | tf_op jit(solution)/shard_map/ppermute | solution.py:57
  58.5 3.2 %collective-permute-done.9.minus = bf16[16,16,256]{2,1,0:T(8,128)(2,1)S(1)} collective-permute-done((bf16[16,16,256]{2,1,0:T(8,128)(2,1)S(1)}, bf16[16,16,256]{2,1,0:T(8,128)(2,1)S(1)}, u32[]{:S(2)}, u32[]{:S(2)}) %collective-permute-start.9) | collective-permute-done | bytes 131104 | tf_op jit(solution)/shard_map/ppermute | solution.py:57
  61.7 2.5 %collective-permute-done.10.cross = bf16[16,16,256]{2,1,0:T(8,128)(2,1)S(1)} collective-permute-done((bf16[16,16,256]{2,1,0:T(8,128)(2,1)S(1)}, bf16[16,16,256]{2,1,0:T(8,128)(2,1)S(1)}, u32[]{:S(2)}, u32[]{:S(2)}) %collective-permute-start.10) | collective-permute-done | bytes 131104 | tf_op jit(solution)/shard_map/ppermute | solution.py:57
  64.2 0.8 %last_sum.1 = f32[16,16,256]{2,1,0:T(8,128)} custom-call(f32[16,16,256]{2,1,0:T(8,128)S(1)} %get-tuple-element.25.keep, f32[16,16,256]{2,1,0:T(8,128)S(1)} %get-tuple-element.35.mine, bf16[16,16,256]{2,1,0:T(8,128)(2,1)S(1)} %collective-permute-done.8.plus, bf16[16,16,256]{2,1,0:T(8,128)(2,1)S(1)} %collective-permute-done.9.minus, ...), custom_call_target="tpu_custom_call" | custom-call | tf_op jit(solution)/shard_map/last_sum/pallas_call | solution.py:309
  (1 shorter events, 0.0 us)
Async XLA Ops:
  0.0 27.0 %copy-start = (s32[16]{0:T(128)S(1)}, s32[16]{0:T(128)}, u32[]{:S(2)}) copy-start(s32[16]{0:T(128)} %sizes.1) | copy-start | bytes 196
  0.0 27.0 %copy-start.2 = (s32[48,1]{0,1:T(1,128)S(1)}, s32[48,1]{0,1:T(1,128)}, u32[]{:S(2)}) copy-start(s32[48,1]{0,1:T(1,128)} %param.12) | copy-start | bytes 580
  0.0 27.0 %copy-start.1 = (s32[48,1]{0,1:T(1,128)S(1)}, s32[48,1]{0,1:T(1,128)}, u32[]{:S(2)}) copy-start(s32[48,1]{0,1:T(1,128)} %param.11) | copy-start | bytes 580
  3.1 23.9 %collective-permute-start = (bf16[16,256,256]{2,1,0:T(8,128)(2,1)S(1)}, bf16[16,256,256]{2,1,0:T(8,128)(2,1)S(1)}, u32[]{:S(2)}, u32[]{:S(2)}) collective-permute-start(bf16[16,256,256]{2,1,0:T(8,128)(2,1)S(1)} %get-tuple-element.24.masked), channel_id=1, source_target_pairs={{0,16},{1,17},{2,18},{3,19},{4,20},{5,21},{6,22},{7,23},{8,24},{9,... | collective-permute-start | bytes 6291464 | tf_op jit(solution)/shard_map/ppermute | solution.py:57
  3.2 30.7 %collective-permute-start.4 = (bf16[7,256,256]{2,1,0:T(8,128)(2,1)S(1)}, bf16[7,256,256]{2,1,0:T(8,128)(2,1)S(1)}, u32[]{:S(2)}, u32[]{:S(2)}) collective-permute-start(bf16[7,256,256]{2,1,0:T(8,128)(2,1)S(1)} %get-tuple-element.29), channel_id=1, source_target_pairs={{16,32},{17,33},{18,34},{19,35},{20,36},{21,37},{22,38},{23,39},{2... | collective-permute-start | bytes 2752520 | tf_op jit(solution)/shard_map/ppermute | solution.py:57
  5.3 18.0 %collective-permute-start.1 = (bf16[3,256,256]{2,1,0:T(8,128)(2,1)S(1)}, bf16[3,256,256]{2,1,0:T(8,128)(2,1)S(1)}, u32[]{:S(2)}, u32[]{:S(2)}) collective-permute-start(bf16[3,256,256]{2,1,0:T(8,128)(2,1)S(1)} %get-tuple-element.28), channel_id=1, source_target_pairs={{16,32},{17,33},{18,34},{19,35},{20,36},{21,37},{22,38},{23,39},{2... | collective-permute-start | bytes 1179656 | tf_op jit(solution)/shard_map/ppermute | solution.py:57
  23.4 9.8 %collective-permute-start.3 = (bf16[3,256,256]{2,1,0:T(8,128)(2,1)S(1)}, bf16[3,256,256]{2,1,0:T(8,128)(2,1)S(1)}, u32[]{:S(2)}, u32[]{:S(2)}) collective-permute-start(bf16[3,256,256]{2,1,0:T(8,128)(2,1)S(1)} %collective-permute-done.1.own), channel_id=1, source_target_pairs={{0,3},{1,2},{2,1},{3,0},{4,7},{5,6},{6,5},{7,4},{8,11},{9,10},{10,... | collective-permute-start | bytes 1179656 | tf_op jit(solution)/shard_map/ppermute | solution.py:57
  26.1 7.8 %collective-permute-start.2 = (bf16[3,256,256]{2,1,0:T(8,128)(2,1)S(1)}, bf16[3,256,256]{2,1,0:T(8,128)(2,1)S(1)}, u32[]{:S(2)}, u32[]{:S(2)}) collective-permute-start(bf16[3,256,256]{2,1,0:T(8,128)(2,1)S(1)} %collective-permute-done.1.own), channel_id=1, source_target_pairs={{0,1},{1,0},{2,3},{3,2},{4,5},{5,4},{6,7},{7,6},{8,9},{9,8},{10,11... | collective-permute-start | bytes 1179656 | tf_op jit(solution)/shard_map/ppermute | solution.py:57
  36.4 9.3 %collective-permute-start.5 = (bf16[16,4,16,256]{3,2,1,0:T(8,128)(2,1)S(1)}, bf16[16,4,16,256]{3,2,1,0:T(8,128)(2,1)S(1)}, u32[]{:S(2)}, u32[]{:S(2)}) collective-permute-start(bf16[16,4,16,256]{3,2,1,0:T(8,128)(2,1)S(1)} %get-tuple-element.32), channel_id=1, source_target_pairs={{0,1},{1,0},{2,3},{3,2},{4,5},{5,4},{6,7},{7,6},{8,9},{9,8},{10,11... | collective-permute-start | bytes 1572872 | tf_op jit(solution)/shard_map/ppermute | solution.py:57
  37.1 16.0 %collective-permute-start.6 = (bf16[16,4,16,256]{3,2,1,0:T(8,128)(2,1)S(1)}, bf16[16,4,16,256]{3,2,1,0:T(8,128)(2,1)S(1)}, u32[]{:S(2)}, u32[]{:S(2)}) collective-permute-start(bf16[16,4,16,256]{3,2,1,0:T(8,128)(2,1)S(1)} %get-tuple-element.33), channel_id=1, source_target_pairs={{0,3},{1,2},{2,1},{3,0},{4,7},{5,6},{6,5},{7,4},{8,11},{9,10},{10,... | collective-permute-start | bytes 1572872 | tf_op jit(solution)/shard_map/ppermute | solution.py:57
  37.8 15.3 %collective-permute-start.7 = (bf16[16,4,16,256]{3,2,1,0:T(8,128)(2,1)S(1)}, bf16[16,4,16,256]{3,2,1,0:T(8,128)(2,1)S(1)}, u32[]{:S(2)}, u32[]{:S(2)}) collective-permute-start(bf16[16,4,16,256]{3,2,1,0:T(8,128)(2,1)S(1)} %get-tuple-element.34), channel_id=1, source_target_pairs={{0,2},{1,3},{2,0},{3,1},{4,6},{5,7},{6,4},{7,5},{8,10},{9,11},{10,... | collective-permute-start | bytes 1572872 | tf_op jit(solution)/shard_map/ppermute | solution.py:57
  53.5 5.1 %collective-permute-start.8 = (bf16[16,16,256]{2,1,0:T(8,128)(2,1)S(1)}, bf16[16,16,256]{2,1,0:T(8,128)(2,1)S(1)}, u32[]{:S(2)}, u32[]{:S(2)}) collective-permute-start(bf16[16,16,256]{2,1,0:T(8,128)(2,1)S(1)} %get-tuple-element.36), channel_id=1, source_target_pairs={{0,4},{1,5},{2,6},{3,7},{4,0},{5,1},{6,2},{7,3},{8,12},{9,13},{10,... | collective-permute-start | bytes 393224 | tf_op jit(solution)/shard_map/ppermute | solution.py:57
  55.1 6.6 %collective-permute-start.9 = (bf16[16,16,256]{2,1,0:T(8,128)(2,1)S(1)}, bf16[16,16,256]{2,1,0:T(8,128)(2,1)S(1)}, u32[]{:S(2)}, u32[]{:S(2)}) collective-permute-start(bf16[16,16,256]{2,1,0:T(8,128)(2,1)S(1)} %get-tuple-element.37), channel_id=1, source_target_pairs={{0,12},{1,13},{2,14},{3,15},{4,8},{5,9},{6,10},{7,11},{8,4},{9,5},... | collective-permute-start | bytes 393224 | tf_op jit(solution)/shard_map/ppermute | solution.py:57
  57.8 6.5 %collective-permute-start.10 = (bf16[16,16,256]{2,1,0:T(8,128)(2,1)S(1)}, bf16[16,16,256]{2,1,0:T(8,128)(2,1)S(1)}, u32[]{:S(2)}, u32[]{:S(2)}) collective-permute-start(bf16[16,16,256]{2,1,0:T(8,128)(2,1)S(1)} %get-tuple-element.38), channel_id=1, source_target_pairs={{0,8},{1,9},{2,10},{3,11},{4,12},{5,13},{6,14},{7,15},{8,0},{9,1},... | collective-permute-start | bytes 393224 | tf_op jit(solution)/shard_map/ppermute | solution.py:57
